TPU v7x, 512 devices: a 4x2x32 block of a 4x8x32 slice. The times are simulated.
512 devices in a mesh: slide: 2 (over y), row: 64 (over z, core), col: 4 (over x).
Axes of the slice: x: 4, y: 2, z: 32, core: 2. Of those that a mesh axis runs over, the one named last changes fastest.
The devices are a block of a 4x8x32 slice.
Arguments:
- features: bfloat16 [896, 1792, 96], P(('slide', 'row'), 'col'), parts along dimension 0, may hold values from -6 to 6
- region_ids: int32 [128, 256, 49], P(('slide', 'row'), 'col'), parts along dimension 0, may hold values from 0 to 1073741823, as said below
- qkv_weight: bfloat16 [96, 288], replicated, may hold values from -0.625 to 0.625
- proj_weight: bfloat16 [96, 96], replicated, may hold values from -0.625 to 0.625
- rel_bias: float32 [169, 3], replicated, may hold values from -5 to 280
- fc1_weight: bfloat16 [96, 384], replicated, may hold values from -0.625 to 0.625
- fc2_weight: bfloat16 [384, 96], replicated, may hold values from -0.3125 to 0.3125
Outputs:
- block_out: bfloat16 [896, 1792, 96], P(('slide', 'row'), 'col'), parts along dimension 0
There are 2 independent parts, one for each index of `slide`. A program takes and returns all parts, laid end to end along the dimension named above; an argument that names none is the same for every part. Nothing has to cross between parts.
Inputs may be any that keep to these rules, and one draw needn't show every extreme that they name: `region_ids`: within each window, each token's id marks the region it belongs to; a window holds at most 4 distinct ids.
All inputs are finite; a program needn't handle non-finite values.
Results may differ from a plain program's by a relative error of at most 0.011.
Values may be sent and summed in bfloat16 or wider, within the bound.
No kernel may reach another device: no remote copies, remote signals or barrier semaphores. Data moves between devices by JAX's collectives and lax.ppermute only.
A program may use at most 64 MiB of HBM per device.

v0:
```python
import jax
import jax.numpy as jnp
import numpy as np
from jax import lax
from jax.experimental import pallas as pl
from jax.experimental.layout import Layout, with_layout_constraint
from jax.experimental.pallas import tpu as pltpu
from jax.sharding import PartitionSpec as P


HEADS = 3
WIN = 7
SHIFT = 3
KEEP = WIN - SHIFT
PAD = 8
KEYS = WIN * PAD
GROUP = 13
LANES = 128
NEG = -1e30
F32 = jnp.float32
BF16 = jnp.bfloat16

epsilon = 1e-05


def moved(value, rows, cols):
    height, width = lax.axis_size("row"), lax.axis_size("col")
    pairs = [
        (r * width + c, (r + rows) % height * width + (c + cols) % width) for r in range(height) for c in range(width)
    ]
    return lax.ppermute(value, ("row", "col"), pairs)


def rowmajor(value):
    return with_layout_constraint(value, Layout(major_to_minor=tuple(range(value.ndim))))


def digits_of(ids):
    rows = jnp.stack([(ids >> (8 * n)) & 255 for n in range(4)])
    return rows.astype(BF16)


def ids_from(digits):
    whole = digits.astype(jnp.int32)
    return sum(whole[n] << (8 * n) for n in range(4))


def strip_with_ids(strip, ids):
    width = strip.shape[-1]
    digits = jnp.pad(digits_of(ids), ((0, 0), (0, width - ids.shape[0])))
    return jnp.concatenate([strip.reshape(-1, width), digits], axis=0)


def layer_norm(values, axis):
    average = jnp.mean(values, axis=axis, keepdims=True)
    centred = values - average
    variance = jnp.mean(centred * centred, axis=axis, keepdims=True)
    return centred * lax.rsqrt(variance + epsilon)


def bias_of(rel_bias, first, rows):
    index = np.full((rows * PAD, KEYS), -1, np.int32)
    for kr in range(WIN):
        for kc in range(WIN):
            for qr in range(rows):
                for qc in range(WIN):
                    index[qr * PAD + qc, kr * PAD + kc] = (qr + first - kr + WIN - 1) * (2 * WIN - 1) + (qc - kc + WIN - 1)
    chosen = jnp.asarray(index)[:, None, :] == jnp.arange(rel_bias.shape[0], dtype=jnp.int32)[None, :, None]
    table = jnp.einsum("qpk,ph->hqk", chosen.astype(F32), rel_bias, precision=lax.Precision.HIGHEST)
    return table.reshape(HEADS * rows * PAD, KEYS)


def slots(ids):
    count = ids.shape[0]
    wide = jnp.pad(ids.reshape(count, WIN, WIN), ((0, 0), (0, 0), (0, PAD - WIN)), constant_values=-1)
    return wide.reshape(count, KEYS)


def attend(tokens, att, att_row, base, first, rows, ids, wqkv, wproj, bias, groups):
    count = rows * PAD
    width = wproj.shape[0]
    head_dim = width // HEADS
    scale = head_dim ** (-0.5)
    lane = lax.broadcasted_iota(jnp.int32, (count, LANES), 1) // head_dim
    blank = jnp.zeros((PAD, width), F32)
    ones = jnp.ones((KEYS, LANES), BF16)

    def by_head(values):
        chosen = values[:count]
        for h in range(1, HEADS):
            chosen = jnp.where(lane == h, values[h * count : (h + 1) * count], chosen)
        return chosen

    def group(g, carry):
        tiles = []
        for w in range(GROUP):
            at = (g * GROUP + w) * WIN + PAD - KEEP
            for r in range(WIN):
                tiles.append(tokens[base + r, pl.ds(at, PAD), :])
            tiles.append(blank)
        windows = jnp.concatenate(tiles, axis=0).astype(BF16)
        qkv = jnp.dot(windows, wqkv[...], preferred_element_type=F32)
        queries = qkv[:, :LANES]
        keys = qkv[:, LANES : 2 * LANES].astype(BF16)
        values = qkv[:, 2 * LANES :].astype(BF16)
        key_ids = ids[g]
        query_ids = key_ids.T[first * PAD : first * PAD + count]
        stride = (WIN + 1) * PAD
        contexts = []
        for w in range(GROUP):
            top = w * stride
            own = queries[top + first * PAD : top + first * PAD + count]
            split = jnp.concatenate([jnp.where(lane == h, own, 0.0) for h in range(HEADS)], axis=0).astype(BF16)
            scores = lax.dot_general(
                split, keys[top : top + KEYS], (((1,), (1,)), ((), ())), preferred_element_type=F32
            )
            scores = scores * scale + bias[...]
            same = query_ids[:, w : w + 1] == key_ids[w : w + 1, :]
            scores = jnp.where(jnp.concatenate([same] * HEADS, axis=0), scores, NEG)
            scores = jnp.exp(scores - jnp.max(scores, axis=1, keepdims=True)).astype(BF16)
            both = jnp.concatenate([values[top : top + KEYS], ones], axis=1)
            mixed = jnp.dot(scores, both, preferred_element_type=F32)
            contexts.append(by_head(mixed[:, :LANES]) / by_head(mixed[:, LANES:]))
        context = jnp.concatenate(contexts, axis=0)[:, :width].astype(BF16)
        branch = jnp.dot(context, wproj[...], preferred_element_type=F32).astype(BF16).astype(F32)
        for w in range(GROUP):
            at = (g * GROUP + w) * WIN + PAD - KEEP
            for r in range(rows):
                top = w * count + r * PAD
                att[att_row + r, pl.ds(at, PAD), :] = branch[top : top + PAD]
        return carry

    lax.fori_loop(0, groups, group, 0, unroll=True)


def block_kernel(own, before, after, left, right, ids_a, ids_b, wqkv, wproj, bias_a, bias_b, fc1, fc2, out, tokens, att):
    tile_rows, width, tile_cols = own.shape
    total = 2 * WIN

    def normed(values, axis):
        return layer_norm(values.astype(F32), axis).astype(BF16).astype(F32)

    for r in range(total):
        if r < KEEP:
            source = before[r]
        elif r < KEEP + WIN:
            source = own[r - KEEP]
        else:
            source = after[r - KEEP - WIN]
        tokens[r, PAD : PAD + tile_cols, :] = normed(source, 0).T
    tokens[:, PAD - KEEP : PAD, :] = normed(left[...], -1)
    tail = jnp.concatenate([normed(right[...], -1), jnp.zeros((total, PAD - SHIFT, width), F32)], axis=1)
    tokens[:, PAD + tile_cols : 2 * PAD + tile_cols, :] = tail
    groups = ids_a.shape[0]
    attend(tokens, att, 0, 0, KEEP, SHIFT, ids_b, wqkv, wproj, bias_b, groups)
    attend(tokens, att, SHIFT, WIN, 0, KEEP, ids_a, wqkv, wproj, bias_a, groups)

    def row(r, carry):
        summed = own[r].astype(F32) + att[r, PAD : PAD + tile_cols, :].T
        second = layer_norm(summed, 0).astype(BF16)
        hidden = jnp.dot(fc1[...], second, preferred_element_type=F32)
        hidden = (hidden * (1.0 + lax.erf(hidden * (0.5**0.5)))).astype(BF16)
        out[r] = (summed + jnp.dot(fc2[...], hidden, preferred_element_type=F32)).astype(BF16)
        return carry

    lax.fori_loop(0, tile_rows, row, 0, unroll=True)


def shards(features, region_ids, qkv_weight, proj_weight, rel_bias, fc1_weight, fc2_weight):
    tile_rows, tile_cols, width = features.shape
    tile = rowmajor(jnp.swapaxes(features, 1, 2))
    count = region_ids.shape[-1]

    def columns(rows, part):
        return jnp.swapaxes(rowmajor(rows[:, :, part]), 1, 2)

    first, last = slice(0, SHIFT), slice(tile_cols - KEEP, tile_cols)
    before = rowmajor(moved(rowmajor(tile[SHIFT:]), 1, 0))
    ids_before = moved(region_ids, 1, 0)
    corner_left = moved(strip_with_ids(columns(tile[SHIFT:], last), region_ids[0, -1]), 1, 1)
    corner_right = moved(columns(tile[SHIFT:], first), 1, -1)
    after = rowmajor(moved(rowmajor(tile[:SHIFT]), -1, 0))
    tall = jnp.concatenate([columns(tile, last), columns(after, last)], axis=0)
    side_left = moved(strip_with_ids(tall, region_ids[0, -1]), 0, 1)
    side_right = moved(jnp.concatenate([columns(tile, first), columns(after, first)], axis=0), 0, -1)

    def split(packed):
        return packed[:-4].reshape(-1, KEEP, width), ids_from(packed[-4:, :count])

    corner_left, ids_corner = split(corner_left)
    side_left, ids_side = split(side_left)
    left = jnp.concatenate([corner_left, side_left], axis=0)
    right = jnp.concatenate([corner_right, side_right], axis=0)
    ids = jnp.concatenate([ids_before, region_ids], axis=0)
    ids = jnp.concatenate([jnp.stack([ids_corner, ids_side])[:, None], ids], axis=1)
    windows = ids.shape[1]
    groups = -(-windows // GROUP)
    ids = slots(ids.reshape(2 * windows, -1)).reshape(2, groups, GROUP, KEYS)
    ids = jnp.pad(ids, ((0, 0), (0, 0), (0, -GROUP % PAD), (0, 0)))
    wqkv = jnp.pad(qkv_weight.reshape(width, 3, width), ((0, 0), (0, 0), (0, LANES - width))).reshape(width, 3 * LANES)
    bias_a = bias_of(rel_bias, 0, KEEP)
    bias_b = bias_of(rel_bias, KEEP, SHIFT)
    result = pl.pallas_call(
        block_kernel,
        out_shape=jax.ShapeDtypeStruct((tile_rows, width, tile_cols), BF16),
        scratch_shapes=[
            pltpu.VMEM((2 * WIN, tile_cols + 2 * PAD, width), F32),
            pltpu.VMEM((tile_rows, tile_cols + 2 * PAD, width), F32),
        ],
        compiler_params=pltpu.CompilerParams(vmem_limit_bytes=48 * 1024 * 1024),
    )(
        tile,
        before,
        after,
        left,
        right,
        ids[1],
        ids[0],
        wqkv,
        proj_weight,
        bias_a,
        bias_b,
        fc1_weight.T,
        (0.5 * fc2_weight).T,
    )
    return jnp.swapaxes(result, 1, 2)


def solution(mesh):
    spec = P(("slide", "row"), "col", None)
    return jax.shard_map(
        shards,
        mesh=mesh,
        in_specs=(spec, spec, P(), P(), P(), P(), P()),
        out_specs=spec,
        check_vma=False,
    )
```

profile of v0, /device:TPU:40, one launch (start us, length us, event | category | flops | bytes accessed | tf_op | source)
XLA Modules:
  0.0 88.7 jit_solution(4405974584130432363)
XLA Ops:
  0.0 1.0 %slice.104 = bf16[4,96,3]{2,1,0:T(8,128)(2,1)S(1)} slice(bf16[7,96,448]{2,1,0:T(8,128)(2,1)} %bitcast.45), slice={[3:7], [0:96], [0:3]} | slice | bytes 4608 | tf_op jit(solution)/shard_map/slice | solution.py:175
  1.1 7.5 %collective-permute-start.4 = (bf16[4,3,96]{2,1,0:T(4,128)(2,1)S(1)}, bf16[4,3,96]{2,1,0:T(4,128)(2,1)S(1)}, u32[]{:S(2)}, u32[]{:S(2)}) collective-permute-start(bf16[4,3,96]{2,1,0:T(4,128)(2,1)S(1)} %bitcast.63), channel_id=1, source_target_pairs={{0,7},{1,4},{2,5},{3,6},{4,11},{5,8},{6,9},{7,10},{8,15},{9,12},{1... | collective-permute-start | bytes 6920 | tf_op jit(solution)/shard_map/ppermute | solution.py:31
  8.6 1.8 %convert_reduce_fusion.3 = (bf16[49]{0:T(256)(128)(2,1)S(1)}, bf16[49]{0:T(256)(128)(2,1)S(1)}, bf16[49]{0:T(256)(128)(2,1)S(1)}, bf16[49]{0:T(256)(128)(2,1)S(1)}) fusion(s32[1,64,49]{1,0,2:T(1,128)} %param.10), kind=kLoop, calls=%fused_computation.20 | loop fusion | flops 588 | bytes 588 | tf_op jit(solution)/shard_map/convert.7
  10.4 1.0 %slice_bitcast_fusion.1 = bf16[4,4,96]{1,2,0:T(8,128)(2,1)S(1)} fusion(bf16[7,96,448]{2,1,0:T(8,128)(2,1)} %bitcast.46), kind=kLoop, calls=%fused_computation.9 | loop fusion | bytes 6144 | tf_op jit(solution)/shard_map/transpose | solution.py:175
  11.5 2.0 %collective-permute-start.2 = (bf16[20,96]{1,0:T(8,128)(2,1)S(1)}, bf16[20,96]{1,0:T(8,128)(2,1)S(1)}, u32[]{:S(2)}, u32[]{:S(2)}) collective-permute-start(bf16[20,96]{1,0:T(8,128)(2,1)S(1)} %pad_maximum_fusion.5), channel_id=1, source_target_pairs={{0,5},{1,6},{2,7},{3,4},{4,9},{5,10},{6,11},{7,8},{8,13},{9,14},{1... | collective-permute-start | bytes 11528 | tf_op jit(solution)/shard_map/ppermute | solution.py:31
  13.5 1.0 %slice.98 = bf16[3,96,448]{2,1,0:T(8,128)(2,1)S(1)} slice(bf16[7,96,448]{2,1,0:T(8,128)(2,1)} %bitcast.47), slice={[0:3], [0:96], [0:448]} | slice | bytes 516096 | tf_op jit(solution)/shard_map/slice | solution.py:182
  14.5 37.4 %collective-permute-start.1 = (bf16[3,96,448]{2,1,0:T(8,128)(2,1)S(1)}, bf16[3,96,448]{2,1,0:T(8,128)(2,1)S(1)}, u32[]{:S(2)}, u32[]{:S(2)}) collective-permute-start(bf16[3,96,448]{2,1,0:T(8,128)(2,1)S(1)} %slice.98), channel_id=1, source_target_pairs={{0,252},{1,253},{2,254},{3,255},{4,0},{5,1},{6,2},{7,3},{8,4},{9,5... | collective-permute-start | bytes 774152 | tf_op jit(solution)/shard_map/ppermute | solution.py:31
  52.0 0.1 slice_bitcast_fusion
  52.2 1.3 %fusion.2 = f32[3,32,56]{2,0,1:T(4,128)S(1)} fusion(s32[32,56]{1,0:T(8,128)S(1)} %copy-done.7, f32[169,3]{0,1:T(4,128)S(1)} %copy-done), kind=kOutput, calls=%fused_computation.4 | convolution fusion | flops 11205376 | bytes 30700 | tf_op jit(solution)/shard_map/qpk,ph->hqk/dot_general | solution.py:69
  53.5 1.1 %fusion.3 = f32[3,24,56]{2,0,1:T(4,128)S(1)} fusion(s32[24,56]{1,0:T(8,128)S(1)} %copy-done.8, f32[169,3]{0,1:T(4,128)S(1)} %copy-done), kind=kOutput, calls=%fused_computation.5 | convolution fusion | flops 8404032 | bytes 23532 | tf_op jit(solution)/shard_map/qpk,ph->hqk/dot_general | solution.py:69
  54.7 0.1 copy.38
  55.0 0.1 copy.42
  55.1 0.1 copy.34
  55.3 0.1 copy.31
  55.4 0.7 collective-permute-done.1.after
  56.3 5.1 %collective-permute-start.5 = (bf16[10,3,96]{2,1,0:T(4,128)(2,1)S(1)}, bf16[10,3,96]{2,1,0:T(4,128)(2,1)S(1)}, u32[]{:S(2)}, u32[]{:S(2)}) collective-permute-start(bf16[10,3,96]{2,1,0:T(4,128)(2,1)S(1)} %pad_maximum_fusion.4), channel_id=1, source_target_pairs={{0,3},{1,0},{2,1},{3,2},{4,7},{5,4},{6,5},{7,6},{8,11},{9,8},{10,9... | collective-permute-start | bytes 17288 | tf_op jit(solution)/shard_map/ppermute | solution.py:31
  61.6 2.1 %collective-permute-start.3 = (bf16[44,96]{1,0:T(8,128)(2,1)S(1)}, bf16[44,96]{1,0:T(8,128)(2,1)S(1)}, u32[]{:S(2)}, u32[]{:S(2)}) collective-permute-start(bf16[44,96]{1,0:T(8,128)(2,1)S(1)} %pad_maximum_fusion.2), channel_id=1, source_target_pairs={{0,1},{1,2},{2,3},{3,0},{4,5},{5,6},{6,7},{7,4},{8,9},{9,10},{10,1... | collective-permute-start | bytes 25352 | tf_op jit(solution)/shard_map/ppermute | solution.py:31
  63.8 4.6 %collective-permute-done.3 = bf16[44,96]{1,0:T(8,128)(2,1)S(1)} collective-permute-done((bf16[44,96]{1,0:T(8,128)(2,1)S(1)}, bf16[44,96]{1,0:T(8,128)(2,1)S(1)}, u32[]{:S(2)}, u32[]{:S(2)}) %collective-permute-start.3) | collective-permute-done | bytes 8480 | tf_op jit(solution)/shard_map/ppermute | solution.py:31
  68.5 0.1 copy.36
  68.6 0.2 add_add_fusion
  68.9 0.2 reshape_reshape.7
  69.1 0.2 copy.37
  69.4 0.3 copy-done.2
  69.6 19.0 %shard_map.91 = bf16[7,96,448]{2,1,0:T(8,128)(2,1)} custom-call(bf16[7,96,448]{2,1,0:T(8,128)(2,1)S(1)} %bitcast.51, bf16[4,96,448]{2,1,0:T(8,128)(2,1)S(1)} %collective-permute-done.before, bf16[3,96,448]{2,1,0:T(8,128)(2,1)S(1)} %collective-permute-done.1.after, bf16[14,4,96]{2,1,0:T(4,128)(2,1)S(1)} %pad_maximum_fusion.left, ...), custom_call_target="tpu_custom_call" | custom-call | tf_op jit(solution)/shard_map/pallas_call | solution.py:203
  (54 shorter events, 1.2 us)
Async XLA Ops:
  0.0 52.2 %copy-start = (f32[169,3]{0,1:T(4,128)S(1)}, f32[169,3]{0,1:T(4,128)}, u32[]{:S(2)}) copy-start(f32[169,3]{0,1:T(4,128)} %param.13) | copy-start | bytes 6088
  0.0 51.9 %copy-start.1 = (bf16[7,448,96]{1,2,0:T(8,128)(2,1)S(1)}, bf16[7,448,96]{1,2,0:T(8,128)(2,1)}, u32[]{:S(2)}) copy-start(bf16[7,448,96]{1,2,0:T(8,128)(2,1)} %param.9) | copy-start | bytes 1806340
  0.0 68.6 %collective-permute-start.6 = (s32[1,64,49]{1,0,2:T(1,128)}, s32[1,64,49]{1,0,2:T(1,128)S(1)}, u32[]{:S(2)}, u32[]{:S(2)}) collective-permute-start(s32[1,64,49]{1,0,2:T(1,128)} %param.10), channel_id=1, source_target_pairs={{0,4},{1,5},{2,6},{3,7},{4,8},{5,9},{6,10},{7,11},{8,12},{9,13},{1... | collective-permute-start | bytes 37640 | tf_op jit(solution)/shard_map/ppermute | solution.py:31
  1.1 62.7 %collective-permute-start.4 = (bf16[4,3,96]{2,1,0:T(4,128)(2,1)S(1)}, bf16[4,3,96]{2,1,0:T(4,128)(2,1)S(1)}, u32[]{:S(2)}, u32[]{:S(2)}) collective-permute-start(bf16[4,3,96]{2,1,0:T(4,128)(2,1)S(1)} %bitcast.63), channel_id=1, source_target_pairs={{0,7},{1,4},{2,5},{3,6},{4,11},{5,8},{6,9},{7,10},{8,15},{9,12},{1... | collective-permute-start | bytes 6920 | tf_op jit(solution)/shard_map/ppermute | solution.py:31
  11.5 43.9 %collective-permute-start.2 = (bf16[20,96]{1,0:T(8,128)(2,1)S(1)}, bf16[20,96]{1,0:T(8,128)(2,1)S(1)}, u32[]{:S(2)}, u32[]{:S(2)}) collective-permute-start(bf16[20,96]{1,0:T(8,128)(2,1)S(1)} %pad_maximum_fusion.5), channel_id=1, source_target_pairs={{0,5},{1,6},{2,7},{3,4},{4,9},{5,10},{6,11},{7,8},{8,13},{9,14},{1... | collective-permute-start | bytes 11528 | tf_op jit(solution)/shard_map/ppermute | solution.py:31
  14.5 37.7 %copy-start.4 = (bf16[384,96]{0,1:T(8,128)(2,1)S(1)}, bf16[384,96]{0,1:T(8,128)(2,1)}, u32[]{:S(2)}) copy-start(bf16[384,96]{0,1:T(8,128)(2,1)} %param.15) | copy-start | bytes 221188
  14.5 37.7 %copy-start.7 = (s32[32,56]{1,0:T(8,128)S(1)}, s32[32,56]{1,0:T(8,128)}, u32[]{:S(2)}) copy-start(s32[32,56]{1,0:T(8,128)} %constant.21.clone) | copy-start | bytes 21508
  14.5 41.6 %collective-permute-start.1 = (bf16[3,96,448]{2,1,0:T(8,128)(2,1)S(1)}, bf16[3,96,448]{2,1,0:T(8,128)(2,1)S(1)}, u32[]{:S(2)}, u32[]{:S(2)}) collective-permute-start(bf16[3,96,448]{2,1,0:T(8,128)(2,1)S(1)} %slice.98), channel_id=1, source_target_pairs={{0,252},{1,253},{2,254},{3,255},{4,0},{5,1},{6,2},{7,3},{8,4},{9,5... | collective-permute-start | bytes 774152 | tf_op jit(solution)/shard_map/ppermute | solution.py:31
  51.9 1.6 %copy-start.8 = (s32[24,56]{1,0:T(8,128)S(1)}, s32[24,56]{1,0:T(8,128)}, u32[]{:S(2)}) copy-start(s32[24,56]{1,0:T(8,128)} %constant.22.clone) | copy-start | bytes 16132
  51.9 17.4 %collective-permute-start = (bf16[4,96,448]{2,1,0:T(8,128)(2,1)S(1)}, bf16[4,96,448]{2,1,0:T(8,128)(2,1)S(1)}, u32[]{:S(2)}, u32[]{:S(2)}) collective-permute-start(bf16[4,96,448]{2,1,0:T(8,128)(2,1)S(1)} %slice.97), channel_id=1, source_target_pairs={{0,4},{1,5},{2,6},{3,7},{4,8},{5,9},{6,10},{7,11},{8,12},{9,13},{1... | collective-permute-start | bytes 1032200 | tf_op jit(solution)/shard_map/ppermute | solution.py:31
  52.2 2.5 %copy-start.5 = (bf16[96,288]{1,0:T(8,128)(2,1)S(1)}, bf16[96,288]{1,0:T(8,128)(2,1)}, u32[]{:S(2)}) copy-start(bf16[96,288]{1,0:T(8,128)(2,1)} %param.11) | copy-start | bytes 165892
  53.5 1.4 %copy-start.6 = (bf16[96,384]{1,0:T(8,128)(2,1)S(1)}, bf16[96,384]{1,0:T(8,128)(2,1)}, u32[]{:S(2)}) copy-start(bf16[96,384]{1,0:T(8,128)(2,1)} %param.14) | copy-start | bytes 221188
  54.9 13.8 %copy-start.3 = (s32[1,64,49]{1,0,2:T(1,128)S(1)}, s32[1,64,49]{1,0,2:T(1,128)}, u32[]{:S(2)}) copy-start(s32[1,64,49]{1,0,2:T(1,128)} %param.10) | copy-start | bytes 37636
  56.3 7.5 %collective-permute-start.5 = (bf16[10,3,96]{2,1,0:T(4,128)(2,1)S(1)}, bf16[10,3,96]{2,1,0:T(4,128)(2,1)S(1)}, u32[]{:S(2)}, u32[]{:S(2)}) collective-permute-start(bf16[10,3,96]{2,1,0:T(4,128)(2,1)S(1)} %pad_maximum_fusion.4), channel_id=1, source_target_pairs={{0,3},{1,0},{2,1},{3,2},{4,7},{5,4},{6,5},{7,6},{8,11},{9,8},{10,9... | collective-permute-start | bytes 17288 | tf_op jit(solution)/shard_map/ppermute | solution.py:31
  61.6 6.8 %collective-permute-start.3 = (bf16[44,96]{1,0:T(8,128)(2,1)S(1)}, bf16[44,96]{1,0:T(8,128)(2,1)S(1)}, u32[]{:S(2)}, u32[]{:S(2)}) collective-permute-start(bf16[44,96]{1,0:T(8,128)(2,1)S(1)} %pad_maximum_fusion.2), channel_id=1, source_target_pairs={{0,1},{1,2},{2,3},{3,0},{4,5},{5,6},{6,7},{7,4},{8,9},{9,10},{10,1... | collective-permute-start | bytes 25352 | tf_op jit(solution)/shard_map/ppermute | solution.py:31
  68.9 0.7 copy-start.2
where the time goes:
time: 89.1 us; the launch traced here: 88.7 us
  starting transfers between devices  54.2 us (61%)
  Pallas kernels  19 us (21%)
  waiting for transfers between devices  5.34 us (6%)
  local copies, waits for them, and re-layouts  5.24 us (6%)
  matrix products  2.41 us (3%)
  other arithmetic  2.11 us (2%)
    ppermute x7, starting transfers between devices, moved(): return lax.ppermute(value, ('row', 'col'), pairs)  54.2 us
    pallas_call x1, Pallas kernels, shards(): pl.pallas_call(block_kernel, out_shape=jax.ShapeDtypeStruct((tile_rows, w...  19 us
    ppermute x7, waiting for transfers between devices, moved(): return lax.ppermute(value, ('row', 'col'), pairs)  5.34 us
    dot_general x2, matrix products, bias_of(): jnp.einsum('qpk,ph->hqk', chosen.astype(F32), rel_bias, precision=lax.Pre...  2.41 us
  transfers between devices with their start and end apart: 7, of which 2 were waited for; matrix products, arithmetic and copies ran while one was open for 11% of the time, Pallas kernels for 0%

commit v1 on v0

v1 whole, which is shorter than its diff:
```python
import jax
import jax.numpy as jnp
import numpy as np
from jax import lax
from jax.experimental import pallas as pl
from jax.experimental.layout import Layout, with_layout_constraint
from jax.experimental.pallas import tpu as pltpu
from jax.sharding import PartitionSpec as P


HEADS = 3
WIN = 7
SHIFT = 3
KEEP = WIN - SHIFT
PAD = 8
KEYS = WIN * PAD
GROUP = 13
LANES = 128
NEG = -1e30
F32 = jnp.float32
BF16 = jnp.bfloat16

epsilon = 1e-05


def moved(value, rows, cols, keep=None):
    height, width = lax.axis_size("row"), lax.axis_size("col")
    pairs = [
        (r * width + c, (r + rows) % height * width + (c + cols) % width)
        for r in range(height)
        for c in range(width)
        if keep is None or keep(r, c)
    ]
    return lax.ppermute(value, ("row", "col"), pairs)


def rowmajor(value):
    return with_layout_constraint(value, Layout(major_to_minor=tuple(range(value.ndim))))


def digits_of(ids):
    rows = jnp.stack([(ids >> (8 * n)) & 255 for n in range(4)])
    return rows.astype(BF16)


def ids_from(digits):
    whole = digits.astype(jnp.int32)
    return sum(whole[n] << (8 * n) for n in range(4))


def layer_norm(values, axis):
    average = jnp.mean(values, axis=axis, keepdims=True)
    centred = values - average
    variance = jnp.mean(centred * centred, axis=axis, keepdims=True)
    return centred * lax.rsqrt(variance + epsilon)


def bias_of(rel_bias):
    index = np.full((KEYS, KEYS), -1, np.int32)
    for kr in range(WIN):
        for kc in range(WIN):
            for qr in range(WIN):
                for qc in range(WIN):
                    index[qr * PAD + qc, kr * PAD + kc] = (qr - kr + WIN - 1) * (2 * WIN - 1) + (qc - kc + WIN - 1)
    chosen = jnp.asarray(index)[:, None, :] == jnp.arange(rel_bias.shape[0], dtype=jnp.int32)[None, :, None]
    return jnp.einsum("qpk,ph->hqk", chosen.astype(F32), rel_bias, precision=lax.Precision.HIGHEST)


def slots(ids, total):
    count = ids.shape[0]
    wide = jnp.pad(ids.reshape(count, WIN, WIN), ((0, 0), (0, 0), (0, PAD - WIN)), constant_values=-1)
    return jnp.pad(wide.reshape(count, KEYS), ((0, total - count), (0, 0)))


def normed(values, axis):
    return layer_norm(values.astype(F32), axis).astype(BF16).astype(F32)


def attend(windows, ids, first, rows, wqkv, wproj, bias):
    count = rows * PAD
    width = wproj.shape[0]
    head_dim = width // HEADS
    scale = head_dim ** (-0.5)
    lane = lax.broadcasted_iota(jnp.int32, (count, LANES), 1) // head_dim
    blank = jnp.zeros((PAD, width), F32)
    ones = jnp.ones((KEYS, LANES), BF16)

    def by_head(values):
        chosen = values[:count]
        for h in range(1, HEADS):
            chosen = jnp.where(lane == h, values[h * count : (h + 1) * count], chosen)
        return chosen

    tokens = jnp.concatenate([tile for window in windows for tile in [*window, blank]], axis=0).astype(BF16)
    qkv = jnp.dot(tokens, wqkv[...], preferred_element_type=F32)
    queries = qkv[:, :LANES]
    keys = qkv[:, LANES : 2 * LANES].astype(BF16)
    values = qkv[:, 2 * LANES :].astype(BF16)
    query_ids = ids.T[first * PAD : first * PAD + count]
    stride = (WIN + 1) * PAD
    contexts = []
    for w in range(len(windows)):
        top = w * stride
        own = queries[top + first * PAD : top + first * PAD + count]
        split = jnp.concatenate([jnp.where(lane == h, own, 0.0) for h in range(HEADS)], axis=0).astype(BF16)
        scores = lax.dot_general(split, keys[top : top + KEYS], (((1,), (1,)), ((), ())), preferred_element_type=F32)
        scores = scores * scale + bias[...]
        same = query_ids[:, w : w + 1] == ids[w : w + 1, :]
        scores = jnp.where(jnp.concatenate([same] * HEADS, axis=0), scores, NEG)
        scores = jnp.exp(scores - jnp.max(scores, axis=1, keepdims=True)).astype(BF16)
        both = jnp.concatenate([values[top : top + KEYS], ones], axis=1)
        mixed = jnp.dot(scores, both, preferred_element_type=F32)
        contexts.append(by_head(mixed[:, :LANES]) / by_head(mixed[:, LANES:]))
    context = jnp.concatenate(contexts, axis=0)[:, :width].astype(BF16)
    return jnp.dot(context, wproj[...], preferred_element_type=F32).astype(BF16).astype(F32)


def attend_row(tokens, att, count, ids, first, rows, wqkv, wproj, bias):
    for start in range(0, count, GROUP):
        members = range(start, min(start + GROUP, count))
        places = [(b + 1) * WIN + PAD - KEEP for b in members]
        windows = [[tokens[r, at : at + PAD, :] for r in range(WIN)] for at in places]
        branch = attend(windows, ids[start : start + 2 * PAD, :], first, rows, wqkv, wproj, bias)
        for w, at in enumerate(places):
            for r in range(rows):
                top = (w * rows + r) * PAD
                att[r, at : at + PAD, :] = branch[top : top + PAD]


def lower_windows(own, after, ids, wqkv, wproj, bias, att, tokens):
    _, tile_cols = own.shape[1:]
    for r in range(WIN):
        source = own[SHIFT + r] if r < KEEP else after[r - KEEP]
        tokens[r, PAD : PAD + tile_cols, :] = normed(source, 0).T
    attend_row(tokens, att, tile_cols // WIN - 1, ids, 0, KEEP, wqkv, wproj, bias)


def early_kernel(late, own, after, ids, wqkv, wproj, bias, att, tokens):
    @pl.when(late[0] == 0)
    def _():
        lower_windows(own, after, ids, wqkv, wproj, bias, att, tokens)


def late_kernel(late, own, after, ids, wqkv, wproj, bias, early, att, tokens):
    @pl.when(late[0] == 0)
    def _():
        att[...] = early[...]

    @pl.when(late[0] != 0)
    def _():
        lower_windows(own, after, ids, wqkv, wproj, bias, att, tokens)


def final_kernel(
    own, before, edge_a, left, right, ids, ids_edge, wqkv, wproj, bias_a, bias_b, fc1, fc2, att_a, out, tokens, att_b, side, rim
):
    tile_rows, width, tile_cols = own.shape
    for r in range(WIN):
        source = before[r] if r < KEEP else own[r - KEEP]
        tokens[r, PAD : PAD + tile_cols, :] = normed(source, 0).T
    halo_left = normed(left[...], -1)
    halo_right = jnp.concatenate([normed(right[...], -1), jnp.zeros((2 * WIN, PAD - SHIFT, width), F32)], axis=1)
    tokens[:, PAD - KEEP : PAD, :] = halo_left[:WIN]
    tokens[:, PAD + tile_cols : 2 * PAD + tile_cols, :] = halo_right[:WIN]
    inner = normed(edge_a[...], -1)
    side[0, :, PAD - KEEP : PAD, :] = halo_left[WIN:]
    side[0, :, PAD:, :] = inner[:, :PAD]
    side[1, :, :PAD, :] = inner[:, PAD:]
    side[1, :, PAD:, :] = halo_right[WIN:]

    attend_row(tokens, att_b, tile_cols // WIN, ids, KEEP, SHIFT, wqkv, wproj, bias_b)
    skip = slice(PAD - KEEP, 2 * PAD - KEEP)
    window = [tokens[r, skip, :] for r in range(WIN)]
    branch = attend([window], ids_edge[:PAD, :], KEEP, SHIFT, wqkv, wproj, bias_b)
    for r in range(SHIFT):
        rim[0, r, skip, :] = branch[r * PAD : (r + 1) * PAD]
        rim[0, r, 2 * PAD - KEEP - 1 : 2 * PAD, :] = att_b[r, 2 * PAD - KEEP - 1 : 2 * PAD, :]
    windows = [[side[n, r, skip, :] for r in range(WIN)] for n in range(2)]
    branch = attend(windows, ids_edge[PAD:, :], 0, KEEP, wqkv, wproj, bias_a)
    for r in range(KEEP):
        low, high = r * PAD, (KEEP + r) * PAD
        rim[0, SHIFT + r, skip, :] = branch[low : low + PAD]
        rim[0, SHIFT + r, 2 * PAD - KEEP - 1 : 2 * PAD, :] = att_a[r, 2 * PAD - KEEP - 1 : 2 * PAD, :]
        rim[1, r, :PAD, :] = att_a[r, tile_cols : tile_cols + PAD, :]
        rim[1, r, skip, :] = branch[high : high + PAD]

    for r in range(tile_rows):
        if r < SHIFT:
            pieces = [rim[0, r, PAD:, :], att_b[r, 2 * PAD : PAD + tile_cols, :]]
        else:
            pieces = [rim[0, r, PAD:, :], att_a[r - SHIFT, 2 * PAD : tile_cols, :], rim[1, r - SHIFT, :PAD, :]]
        summed = own[r].astype(F32) + jnp.concatenate(pieces, axis=0).T
        second = layer_norm(summed, 0).astype(BF16)
        hidden = jnp.dot(fc1[...], second, preferred_element_type=F32)
        hidden = (hidden * (1.0 + lax.erf(hidden * (0.5**0.5)))).astype(BF16)
        out[r] = (summed + jnp.dot(fc2[...], hidden, preferred_element_type=F32)).astype(BF16)


def shards(features, region_ids, qkv_weight, proj_weight, rel_bias, fc1_weight, fc2_weight):
    tile_rows, tile_cols, width = features.shape
    tile = rowmajor(jnp.swapaxes(features, 1, 2))
    count = region_ids.shape[-1]
    windows = region_ids.shape[1]
    own_ids = region_ids[0]
    height = lax.axis_size("row")
    row, col = lax.axis_index("row"), lax.axis_index("col")

    def in_wrap(r, c):
        return r == 0 or r == height - 1 or (r == 1 and c == 0)

    late = (row >= height - 2) | ((row == 0) & (col == 0))
    late = late.astype(jnp.int32).reshape(1)

    def columns(rows, part):
        return jnp.swapaxes(rowmajor(rows[:, :, part]), 1, 2)

    first, last = slice(0, SHIFT), slice(tile_cols - KEEP, tile_cols)
    room = windows + 2 * PAD
    wqkv = jnp.pad(qkv_weight.reshape(width, 3, width), ((0, 0), (0, 0), (0, LANES - width))).reshape(width, 3 * LANES)
    bias = bias_of(rel_bias)
    bias_a = bias[:, : KEEP * PAD].reshape(HEADS * KEEP * PAD, KEYS)
    bias_b = bias[:, KEEP * PAD :].reshape(HEADS * SHIFT * PAD, KEYS)
    ids_a = slots(own_ids, room)
    smem = pl.BlockSpec(memory_space=pltpu.SMEM)
    vmem = pl.BlockSpec(memory_space=pltpu.VMEM)
    att_shape = jax.ShapeDtypeStruct((KEEP, tile_cols + 2 * PAD, width), F32)
    token_scratch = pltpu.VMEM((WIN, tile_cols + 2 * PAD, width), F32)
    params = pltpu.CompilerParams(vmem_limit_bytes=40 * 1024 * 1024)

    def call(kernel, operands):
        return pl.pallas_call(
            kernel,
            out_shape=att_shape,
            in_specs=[smem] + [vmem] * (len(operands) - 1),
            out_specs=vmem,
            scratch_shapes=[token_scratch],
            compiler_params=params,
        )(*operands)

    before = rowmajor(moved(rowmajor(tile[SHIFT:]), 1, 0))
    ids_before = moved(region_ids, 1, 0)
    after_main = rowmajor(moved(rowmajor(tile[:SHIFT]), -1, 0, lambda r, c: not in_wrap(r, c)))
    att = call(early_kernel, [late, tile, after_main, ids_a, wqkv, proj_weight, bias_a])
    after_wrap = rowmajor(moved(rowmajor(tile[:SHIFT]), -1, 0, in_wrap))

    def sides(part):
        after = jnp.where(late[0] != 0, columns(after_wrap, part), columns(after_main, part))
        return jnp.concatenate([columns(before, part), columns(tile, part), after], axis=0)

    digits = jnp.concatenate([digits_of(ids_before[0, -1]), digits_of(own_ids[-1])], axis=0)
    digits = jnp.pad(digits, ((0, 0), (0, width - count)))
    left = moved(jnp.concatenate([sides(last).reshape(-1, width), digits], axis=0), 0, 1)
    right = moved(sides(first), 0, -1)
    att = call(late_kernel, [late, tile, after_wrap, ids_a, wqkv, proj_weight, bias_a, att])

    ids_b = slots(ids_before[0], room)
    digits = left[-8:, :count]
    ids_edge = slots(jnp.stack([ids_from(digits[:4]), ids_from(digits[4:]), own_ids[-1]]), 3)
    ids_edge = jnp.concatenate([jnp.pad(ids_edge[:1], ((0, PAD - 1), (0, 0))), jnp.pad(ids_edge[1:], ((0, PAD - 2), (0, 0)))])
    left = left[:-8].reshape(2 * WIN, KEEP, width)

    def inner(rows):
        return jnp.concatenate([columns(rows, slice(0, PAD)), columns(rows, slice(tile_cols - PAD, tile_cols))], axis=1)

    edge_a = jnp.concatenate([inner(tile[SHIFT:]), jnp.where(late[0] != 0, inner(after_wrap), inner(after_main))], axis=0)
    result = pl.pallas_call(
        final_kernel,
        out_shape=jax.ShapeDtypeStruct((tile_rows, width, tile_cols), BF16),
        scratch_shapes=[
            token_scratch,
            pltpu.VMEM((SHIFT, tile_cols + 2 * PAD, width), F32),
            pltpu.VMEM((2, WIN, 2 * PAD, width), F32),
            pltpu.VMEM((2, WIN, 2 * PAD, width), F32),
        ],
        compiler_params=params,
    )(
        tile,
        before,
        edge_a,
        left,
        right,
        ids_b,
        ids_edge,
        wqkv,
        proj_weight,
        bias_a,
        bias_b,
        fc1_weight.T,
        (0.5 * fc2_weight).T,
        att,
    )
    return jnp.swapaxes(result, 1, 2)


def solution(mesh):
    spec = P(("slide", "row"), "col", None)
    return jax.shard_map(
        shards,
        mesh=mesh,
        in_specs=(spec, spec, P(), P(), P(), P(), P()),
        out_specs=spec,
        check_vma=False,
    )
```

time: 89.1 us -> 89 us (level)
  waiting for transfers between devices: 5.34 us -> 1.52 us
  local copies, waits for them, and re-layouts: 5.24 us -> 7.01 us
  Pallas kernels: 19 us -> 19.9 us
    ppermute x7 -> x6, waiting for transfers between devices: 5.34 us -> 1.52 us  [moved(): return lax.ppermute(value, ('row', 'col'), pairs)]
    slice x3 -> x11, local copies, waits for them, and re-layouts: 0.99 us -> 2.31 us  [the longest x1 1.06 us: shards(): after_wrap = rowmajor(moved(rowmajor(tile[:SHIFT]), -1, 0, in_wrap))]
    transpose x6 -> x4, local copies, waits for them, and re-layouts: 1.54 us -> 0.47 us  [columns(): return jnp.swapaxes(rowmajor(rows[:, :, part]), 1, 2)]
    slice x1, local copies, waits for them, and re-layouts: 0.03 us -> 1.03 us  [shards(): before = rowmajor(moved(rowmajor(tile[SHIFT:]), 1, 0))]
    pallas_call x1 -> x3, Pallas kernels: 19 us -> 19.9 us  [the longest x2 10.1 us: call(): pl.pallas_call(kernel, out_shape=att_shape, in_specs=[smem] + [vmem] * (l...]
    ppermute x7 -> x6, starting transfers between devices: 54.2 us -> 54.9 us  [moved(): return lax.ppermute(value, ('row', 'col'), pairs)]
    another operation x2 -> x3, other arithmetic: 1.77 us -> 2.05 us
    dot_general x2 -> x1, matrix products: 2.41 us -> 2.44 us  [bias_of(): jnp.einsum('qpk,ph->hqk', chosen.astype(F32), rel_bias, precision=lax.Pre...]
  transfers between devices with their start and end apart: 7 -> 6, of which waited for: 2 -> 1; matrix products, arithmetic and copies ran while one was open for 11% -> 12% of each run, Pallas kernels for 0% -> 11%
where the time goes in v1:
time: 89 us; the launch traced here: 88.7 us
  starting transfers between devices  54.9 us (62%)
  Pallas kernels  19.9 us (22%)
  local copies, waits for them, and re-layouts  7.01 us (8%)
  other arithmetic  2.45 us (3%)
  matrix products  2.44 us (3%)
  waiting for transfers between devices  1.52 us (2%)
    ppermute x6, starting transfers between devices, moved(): return lax.ppermute(value, ('row', 'col'), pairs)  54.9 us
    pallas_call x2, Pallas kernels, call(): pl.pallas_call(kernel, out_shape=att_shape, in_specs=[smem] + [vmem] * (l...  10.1 us
    pallas_call x1, Pallas kernels, shards(): pl.pallas_call(final_kernel, out_shape=jax.ShapeDtypeStruct((tile_rows, w...  9.83 us
    dot_general x1, matrix products, bias_of(): jnp.einsum('qpk,ph->hqk', chosen.astype(F32), rel_bias, precision=lax.Pre...  2.44 us
    another operation x2, other arithmetic  2.04 us
  transfers between devices with their start and end apart: 6, of which 1 were waited for; matrix products, arithmetic and copies ran while one was open for 12% of the time, Pallas kernels for 11%

profile of v1, /device:TPU:40, one launch (start us, length us, event | category | flops | bytes accessed | tf_op | source)
XLA Modules:
  0.0 88.7 jit_solution(4425329240865699952)
XLA Ops:
  0.0 1.1 %slice.152 = bf16[3,96,448]{2,1,0:T(8,128)(2,1)S(1)} slice(bf16[7,96,448]{2,1,0:T(8,128)(2,1)} %bitcast.49), slice={[0:3], [0:96], [0:448]} | slice | bytes 516096 | tf_op jit(solution)/shard_map/slice | solution.py:244
  1.1 45.0 %collective-permute-start.1 = (bf16[3,96,448]{2,1,0:T(8,128)(2,1)S(1)}, bf16[3,96,448]{2,1,0:T(8,128)(2,1)S(1)}, u32[]{:S(2)}, u32[]{:S(2)}) collective-permute-start(bf16[3,96,448]{2,1,0:T(8,128)(2,1)S(1)} %slice.152), channel_id=1, source_target_pairs={{0,252},{1,253},{2,254},{3,255},{4,0},{252,248},{253,249},{254,250... | collective-permute-start | bytes 774152 | tf_op jit(solution)/shard_map/ppermute | solution.py:34
  46.1 0.7 collective-permute-start.2
  46.8 1.0 %slice.149 = bf16[4,96,448]{2,1,0:T(8,128)(2,1)S(1)} slice(bf16[7,96,448]{2,1,0:T(8,128)(2,1)} %bitcast.50), slice={[3:7], [0:96], [0:448]} | slice | bytes 688128 | tf_op jit(solution)/shard_map/slice | solution.py:240
  48.0 1.0 %slice_reduce_fusion = s32[49]{0:T(128)S(1)} fusion(s32[1,64,49]{1,0,2:T(1,128)S(1)} %copy-done.3), kind=kLoop, calls=%fused_computation.36 | loop fusion | bytes 392 | tf_op jit(solution)/shard_map/slice | solution.py:250
  49.0 1.0 %convert_reduce_fusion = (bf16[49]{0:T(256)(128)(2,1)S(1)}, bf16[49]{0:T(256)(128)(2,1)S(1)}, bf16[49]{0:T(256)(128)(2,1)S(1)}, bf16[49]{0:T(256)(128)(2,1)S(1)}) fusion(s32[1,64,49]{1,0,2:T(1,128)S(1)} %copy-done.3), kind=kLoop, calls=%fused_computation.14 | loop fusion | flops 588 | bytes 588 | tf_op jit(solution)/shard_map/convert.4
  50.0 0.1 slice_bitcast_fusion
  50.4 2.4 %fusion.2 = f32[3,56,56]{2,0,1:T(4,128)S(1)} fusion(s32[56,56]{1,0:T(8,128)S(1)} %copy-done.6, f32[169,3]{0,1:T(4,128)S(1)} %copy-done), kind=kOutput, calls=%fused_computation.3 | convolution fusion | flops 19609408 | bytes 52204 | tf_op jit(solution)/shard_map/qpk,ph->hqk/dot_general | solution.py:66
  53.2 0.1 copy.56
  53.3 0.1 copy.62.wqkv
  53.4 1.0 %copy.60 = bf16[96,384]{0,1:T(8,128)(2,1)S(1)} copy(bf16[96,384]{1,0:T(8,128)(2,1)} %param.13) | data formatting | bytes 147456 | tf_op args[5]
  54.5 0.1 copy.52
  54.6 0.1 copy.49
  55.0 1.0 %convert_reduce_fusion.4 = (bf16[49]{0:T(256)(128)(2,1)S(1)}, bf16[49]{0:T(256)(128)(2,1)S(1)}, bf16[49]{0:T(256)(128)(2,1)S(1)}, bf16[49]{0:T(256)(128)(2,1)S(1)}) fusion(s32[1,64,49]{1,0,2:T(1,128)S(1)} %collective-permute-done.3), kind=kLoop, calls=%fused_computation.18 | loop fusion | flops 588 | bytes 588 | tf_op jit(solution)/shard_map/convert.12
  56.5 0.1 fusion.8
  56.7 0.1 fusion.3
  57.0 0.1 copy.50
  57.3 10.1 %shard_map.83.att_a = f32[4,464,96]{2,1,0:T(8,128)S(1)} custom-call(s32[1]{0:T(128)} %bitcast.24.late, bf16[7,96,448]{2,1,0:T(8,128)(2,1)S(1)} %bitcast.55, bf16[3,96,448]{2,1,0:T(8,128)(2,1)S(1)} %collective-permute-done.1.after, s32[80,56]{1,0:T(8,128)S(1)} %pad.42.ids, bf16[96,384]{1,0:T(8,128)(2,1)S(1)} %copy.62.wqkv, bf16[96,96]{1,0:T(8,128)(2,1)S(1)} %copy-done.2, ...), custom_call_target="tpu_custom_call" | custom-call | tf_op jit(solution)/shard_map/pallas_call | solution.py:231
  67.4 0.1 copy.51
  67.6 0.1 copy.48
  67.8 5.4 %collective-permute-start.4 = (bf16[64,96]{1,0:T(8,128)(2,1)S(1)}, bf16[64,96]{1,0:T(8,128)(2,1)S(1)}, u32[]{:S(2)}, u32[]{:S(2)}) collective-permute-start(bf16[64,96]{1,0:T(8,128)(2,1)S(1)} %fusion.5), channel_id=1, source_target_pairs={{0,1},{1,2},{2,3},{3,0},{4,5},{5,6},{6,7},{7,4},{8,9},{9,10},{10,1... | collective-permute-start | bytes 36872 | tf_op jit(solution)/shard_map/ppermute | solution.py:34
  73.2 3.7 %collective-permute-start.5 = (bf16[14,3,96]{2,1,0:T(4,128)(2,1)S(1)}, bf16[14,3,96]{2,1,0:T(4,128)(2,1)S(1)}, u32[]{:S(2)}, u32[]{:S(2)}) collective-permute-start(bf16[14,3,96]{2,1,0:T(4,128)(2,1)S(1)} %pad_maximum_fusion.2), channel_id=1, source_target_pairs={{0,3},{1,0},{2,1},{3,2},{4,7},{5,4},{6,5},{7,6},{8,11},{9,8},{10,9... | collective-permute-start | bytes 24200 | tf_op jit(solution)/shard_map/ppermute | solution.py:34
  77.3 1.5 %collective-permute-done.5.right = bf16[14,3,96]{2,1,0:T(4,128)(2,1)S(1)} collective-permute-done((bf16[14,3,96]{2,1,0:T(4,128)(2,1)S(1)}, bf16[14,3,96]{2,1,0:T(4,128)(2,1)S(1)}, u32[]{:S(2)}, u32[]{:S(2)}) %collective-permute-start.5) | collective-permute-done | bytes 8096 | tf_op jit(solution)/shard_map/ppermute | solution.py:34
  78.9 9.8 %shard_map.84 = bf16[7,96,448]{2,1,0:T(8,128)(2,1)} custom-call(bf16[7,96,448]{2,1,0:T(8,128)(2,1)S(1)} %bitcast.56, bf16[4,96,448]{2,1,0:T(8,128)(2,1)S(1)} %collective-permute-done.before, bf16[7,16,96]{2,1,0:T(8,128)(2,1)S(1)} %pad_maximum_fusion.edge_a, bf16[14,4,96]{2,1,0:T(4,128)(2,1)S(1)} %bitcast.62, ...), custom_call_target="tpu_custom_call" | custom-call | tf_op jit(solution)/shard_map/pallas_call | solution.py:266
  (72 shorter events, 2.3 us)
Async XLA Ops:
  0.0 50.4 %copy-start = (f32[169,3]{0,1:T(4,128)S(1)}, f32[169,3]{0,1:T(4,128)}, u32[]{:S(2)}) copy-start(f32[169,3]{0,1:T(4,128)} %param.12) | copy-start | bytes 6088
  0.0 50.0 %copy-start.1 = (bf16[7,448,96]{1,2,0:T(8,128)(2,1)S(1)}, bf16[7,448,96]{1,2,0:T(8,128)(2,1)}, u32[]{:S(2)}) copy-start(bf16[7,448,96]{1,2,0:T(8,128)(2,1)} %param.8) | copy-start | bytes 1806340
  0.0 47.9 %copy-start.3 = (s32[1,64,49]{1,0,2:T(1,128)S(1)}, s32[1,64,49]{1,0,2:T(1,128)}, u32[]{:S(2)}) copy-start(s32[1,64,49]{1,0,2:T(1,128)} %param.9) | copy-start | bytes 37636
  1.1 49.3 %copy-start.4 = (bf16[384,96]{0,1:T(8,128)(2,1)S(1)}, bf16[384,96]{0,1:T(8,128)(2,1)}, u32[]{:S(2)}) copy-start(bf16[384,96]{0,1:T(8,128)(2,1)} %param.14) | copy-start | bytes 221188
  1.1 49.3 %copy-start.6 = (s32[56,56]{1,0:T(8,128)S(1)}, s32[56,56]{1,0:T(8,128)}, u32[]{:S(2)}) copy-start(s32[56,56]{1,0:T(8,128)} %constant.30.clone) | copy-start | bytes 37636
  1.1 55.1 %collective-permute-start.1 = (bf16[3,96,448]{2,1,0:T(8,128)(2,1)S(1)}, bf16[3,96,448]{2,1,0:T(8,128)(2,1)S(1)}, u32[]{:S(2)}, u32[]{:S(2)}) collective-permute-start(bf16[3,96,448]{2,1,0:T(8,128)(2,1)S(1)} %slice.152), channel_id=1, source_target_pairs={{0,252},{1,253},{2,254},{3,255},{4,0},{252,248},{253,249},{254,250... | collective-permute-start | bytes 774152 | tf_op jit(solution)/shard_map/ppermute | solution.py:34
  46.1 10.4 %collective-permute-start.2 = (bf16[3,96,448]{2,1,0:T(8,128)(2,1)S(1)}, bf16[3,96,448]{2,1,0:T(8,128)(2,1)S(1)}, u32[]{:S(2)}, u32[]{:S(2)}) collective-permute-start(bf16[3,96,448]{2,1,0:T(8,128)(2,1)S(1)} %slice.152), channel_id=1, source_target_pairs={{5,1},{6,2},{7,3},{8,4},{9,5},{10,6},{11,7},{12,8},{13,9},{14,10},... | collective-permute-start | bytes 774152 | tf_op jit(solution)/shard_map/ppermute | solution.py:34
  46.8 8.2 %collective-permute-start.3 = (s32[1,64,49]{1,0,2:T(1,128)}, s32[1,64,49]{1,0,2:T(1,128)S(1)}, u32[]{:S(2)}, u32[]{:S(2)}) collective-permute-start(s32[1,64,49]{1,0,2:T(1,128)} %param.9), channel_id=1, source_target_pairs={{0,4},{1,5},{2,6},{3,7},{4,8},{5,9},{6,10},{7,11},{8,12},{9,13},{1... | collective-permute-start | bytes 37640 | tf_op jit(solution)/shard_map/ppermute | solution.py:34
  47.9 19.5 %collective-permute-start = (bf16[4,96,448]{2,1,0:T(8,128)(2,1)S(1)}, bf16[4,96,448]{2,1,0:T(8,128)(2,1)S(1)}, u32[]{:S(2)}, u32[]{:S(2)}) collective-permute-start(bf16[4,96,448]{2,1,0:T(8,128)(2,1)S(1)} %slice.149), channel_id=1, source_target_pairs={{0,4},{1,5},{2,6},{3,7},{4,8},{5,9},{6,10},{7,11},{8,12},{9,13},{1... | collective-permute-start | bytes 1032200 | tf_op jit(solution)/shard_map/ppermute | solution.py:34
  50.3 2.8 %copy-start.5 = (bf16[96,288]{1,0:T(8,128)(2,1)S(1)}, bf16[96,288]{1,0:T(8,128)(2,1)}, u32[]{:S(2)}) copy-start(bf16[96,288]{1,0:T(8,128)(2,1)} %param.10) | copy-start | bytes 165892
  56.1 1.2 %copy-start.2 = (bf16[96,96]{1,0:T(8,128)(2,1)S(1)}, bf16[96,96]{1,0:T(8,128)(2,1)}, u32[]{:S(2)}) copy-start(bf16[96,96]{1,0:T(8,128)(2,1)} %wproj.5) | copy-start | bytes 55300
  67.8 9.1 %collective-permute-start.4 = (bf16[64,96]{1,0:T(8,128)(2,1)S(1)}, bf16[64,96]{1,0:T(8,128)(2,1)S(1)}, u32[]{:S(2)}, u32[]{:S(2)}) collective-permute-start(bf16[64,96]{1,0:T(8,128)(2,1)S(1)} %fusion.5), channel_id=1, source_target_pairs={{0,1},{1,2},{2,3},{3,0},{4,5},{5,6},{6,7},{7,4},{8,9},{9,10},{10,1... | collective-permute-start | bytes 36872 | tf_op jit(solution)/shard_map/ppermute | solution.py:34
  73.2 5.6 %collective-permute-start.5 = (bf16[14,3,96]{2,1,0:T(4,128)(2,1)S(1)}, bf16[14,3,96]{2,1,0:T(4,128)(2,1)S(1)}, u32[]{:S(2)}, u32[]{:S(2)}) collective-permute-start(bf16[14,3,96]{2,1,0:T(4,128)(2,1)S(1)} %pad_maximum_fusion.2), channel_id=1, source_target_pairs={{0,3},{1,0},{2,1},{3,2},{4,7},{5,4},{6,5},{7,6},{8,11},{9,8},{10,9... | collective-permute-start | bytes 24200 | tf_op jit(solution)/shard_map/ppermute | solution.py:34

commit v2 on v1

v2 whole, which is shorter than its diff:
```python
import functools

import jax
import jax.numpy as jnp
import numpy as np
from jax import lax
from jax.experimental import pallas as pl
from jax.experimental.layout import Layout, with_layout_constraint
from jax.experimental.pallas import tpu as pltpu
from jax.sharding import PartitionSpec as P


HEADS = 3
WIN = 7
SHIFT = 3
KEEP = WIN - SHIFT
PAD = 8
KEYS = WIN * PAD
GROUP = 13
LANES = 128
NEG = -1e30
F32 = jnp.float32
BF16 = jnp.bfloat16

epsilon = 1e-05


def moved(value, rows, cols, keep=None):
    slides, height, width = lax.axis_size("slide"), lax.axis_size("row"), lax.axis_size("col")
    pairs = [
        ((s * height + r) * width + c, (s * height + (r + rows) % height) * width + (c + cols) % width)
        for s in range(slides)
        for r in range(height)
        for c in range(width)
        if keep is None or keep(s, r, c)
    ]
    return lax.ppermute(value, ("slide", "row", "col"), pairs)


def rowmajor(value):
    return with_layout_constraint(value, Layout(major_to_minor=tuple(range(value.ndim))))


def layer_norm(values, axis):
    average = jnp.mean(values, axis=axis, keepdims=True)
    centred = values - average
    variance = jnp.mean(centred * centred, axis=axis, keepdims=True)
    return centred * lax.rsqrt(variance + epsilon)


def bias_onehot():
    span = 2 * WIN - 1
    table = np.zeros((span * span, PAD, LANES), np.float32)
    for cq in range(WIN):
        for j in range(span):
            for ck in range(WIN):
                table[(span - 1 - j) * span + cq - ck + WIN - 1, cq, j * PAD + ck] = 1.0
    return table.reshape(span * span, PAD * LANES)


def fill_strip(rel_bias, onehot, strip):
    rest = rel_bias[...]
    picked = 0.0
    for _ in range(3):
        part = lax.reduce_precision(rest, exponent_bits=8, mantissa_bits=7)
        rest = rest - part
        picked = picked + jnp.dot(part.astype(BF16), onehot[...], preferred_element_type=F32)
    for cq in range(PAD):
        strip[:, cq, :] = picked[:, cq * LANES : (cq + 1) * LANES]


def bias_tiles(strip, first, rows):
    tiles = []
    for h in range(HEADS):
        for r in range(first, first + rows):
            tiles.append(strip[h, :, (WIN - 1 - r) * PAD : (WIN - 1 - r) * PAD + KEYS])
    return jnp.concatenate(tiles, axis=0)


def spread_ids(ids, spread):
    spread[...] = jnp.full(spread.shape, -1, jnp.int32)
    for r in range(WIN):
        spread[r * PAD : r * PAD + WIN, : ids.shape[2]] = ids[r * WIN : (r + 1) * WIN, 0, :]
    return spread[...]


def widen(weight, wide):
    width = weight.shape[0]
    wide[...] = jnp.zeros(wide.shape, BF16)
    for n in range(3):
        wide[:, n * LANES : n * LANES + width] = weight[:, n * width : (n + 1) * width]


def normed(values, axis):
    return layer_norm(values.astype(F32), axis).astype(BF16).astype(F32)


def attend(windows, ids_t, first, rows, wqkv, wproj, bias):
    count = rows * PAD
    width = wproj.shape[0]
    head_dim = width // HEADS
    scale = head_dim ** (-0.5)
    lane = lax.broadcasted_iota(jnp.int32, (count, LANES), 1) // head_dim
    blank = jnp.zeros((PAD, width), F32)
    ones = jnp.ones((KEYS, LANES), BF16)

    def by_head(values):
        chosen = values[:count]
        for h in range(1, HEADS):
            chosen = jnp.where(lane == h, values[h * count : (h + 1) * count], chosen)
        return chosen

    tokens = jnp.concatenate([tile for window in windows for tile in [*window, blank]], axis=0).astype(BF16)
    qkv = jnp.dot(tokens, wqkv[...], preferred_element_type=F32)
    queries = qkv[:, :LANES]
    keys = qkv[:, LANES : 2 * LANES].astype(BF16)
    values = qkv[:, 2 * LANES :].astype(BF16)
    ids = ids_t.T
    query_ids = ids_t[first * PAD : first * PAD + count]
    stride = (WIN + 1) * PAD
    contexts = []
    for w in range(len(windows)):
        top = w * stride
        own = queries[top + first * PAD : top + first * PAD + count]
        split = jnp.concatenate([jnp.where(lane == h, own, 0.0) for h in range(HEADS)], axis=0).astype(BF16)
        scores = lax.dot_general(split, keys[top : top + KEYS], (((1,), (1,)), ((), ())), preferred_element_type=F32)
        scores = scores * scale + bias
        same = query_ids[:, w : w + 1] == ids[w : w + 1, :]
        scores = jnp.where(jnp.concatenate([same] * HEADS, axis=0), scores, NEG)
        scores = jnp.exp(scores - jnp.max(scores, axis=1, keepdims=True)).astype(BF16)
        both = jnp.concatenate([values[top : top + KEYS], ones], axis=1)
        mixed = jnp.dot(scores, both, preferred_element_type=F32)
        contexts.append(by_head(mixed[:, :LANES]) / by_head(mixed[:, LANES:]))
    context = jnp.concatenate(contexts, axis=0)[:, :width].astype(BF16)
    return jnp.dot(context, wproj[...], preferred_element_type=F32).astype(BF16).astype(F32)


def attend_row(tokens, att, count, ids_t, first, rows, wqkv, wproj, bias):
    for start in range(0, count, GROUP):
        members = range(start, min(start + GROUP, count))
        places = [(b + 1) * WIN + PAD - KEEP for b in members]
        windows = [[tokens[r, at : at + PAD, :] for r in range(WIN)] for at in places]
        branch = attend(windows, ids_t[:, start : start + 2 * PAD], first, rows, wqkv, wproj, bias)
        for w, at in enumerate(places):
            for r in range(rows):
                top = (w * rows + r) * PAD
                att[r, at : at + PAD, :] = branch[top : top + PAD]


def lower_windows(own, after, ids, weight, wproj, rel_bias, onehot, att, tokens, wqkv, strip, spread):
    _, tile_cols = own.shape[1:]
    widen(weight, wqkv)
    fill_strip(rel_bias, onehot, strip)
    bias = bias_tiles(strip, 0, KEEP)
    ids_t = spread_ids(ids, spread)
    for r in range(WIN):
        source = own[SHIFT + r] if r < KEEP else after[r - KEEP]
        tokens[r, PAD : PAD + tile_cols, :] = normed(source, 0).T
    attend_row(tokens, att, tile_cols // WIN - 1, ids_t, 0, KEEP, wqkv, wproj, bias)


def early_kernel(late, *refs):
    @pl.when(late[0] == 0)
    def _():
        lower_windows(*refs)


def late_kernel(late, early, *refs):
    @pl.when(late[0] == 0)
    def _():
        refs[7][...] = early[...]

    @pl.when(late[0] != 0)
    def _():
        lower_windows(*refs)


def pack_kernel(late, own, before, after_main, after_wrap, ids, ids_before, left, right, spread):
    tile_cols = own.shape[2]
    for r in range(2 * WIN):
        if r < KEEP:
            source = before[r]
        elif r < KEEP + WIN:
            source = own[r - KEEP]
        else:
            source = jnp.where(late[0] != 0, after_wrap[r - KEEP - WIN], after_main[r - KEEP - WIN])
        source = source.astype(F32)
        right[r] = source[:, :LANES].T[:PAD].astype(BF16)
        tail = tile_cols // LANES * LANES
        left[r] = source[:, tail:].T[tile_cols - tail - PAD :].astype(BF16)
    columns = [spread_ids(each, spread)[:, each.shape[2] - 1 : each.shape[2]] for each in (ids_before, ids)]
    lane = lax.broadcasted_iota(jnp.int32, (KEYS, own.shape[1]), 1)
    chosen = jnp.where(lane < 4, columns[0], columns[1])
    digits = ((chosen >> (8 * (lane & 3))) & 255).astype(F32)
    for r in range(WIN):
        left[2 * WIN + r] = digits[r * PAD : (r + 1) * PAD].astype(BF16)


def final_kernel(
    late,
    own,
    before,
    after_main,
    after_wrap,
    left,
    right,
    ids,
    ids_before,
    weight,
    wproj,
    rel_bias,
    onehot,
    fc1,
    fc2,
    att_a,
    out,
    tokens,
    wqkv,
    strip,
    spread,
    att_b,
    side,
    rim,
):
    tile_rows, _, tile_cols = own.shape
    widen(weight, wqkv)
    fill_strip(rel_bias, onehot, strip)
    bias_a = bias_tiles(strip, 0, KEEP)
    bias_b = bias_tiles(strip, KEEP, SHIFT)
    for r in range(WIN):
        source = before[r] if r < KEEP else own[r - KEEP]
        tokens[r, PAD : PAD + tile_cols, :] = normed(source, 0).T
    halo_left = normed(left[: 2 * WIN], -1)
    halo_right = normed(right[...], -1)
    tokens[:, :PAD, :] = halo_left[:WIN]
    tokens[:, PAD + tile_cols :, :] = halo_right[:WIN]
    side[0, :, :PAD, :] = halo_left[WIN:]
    side[1, :, PAD:, :] = halo_right[WIN:]
    tail = tile_cols // LANES * LANES
    for r in range(WIN):
        if r < KEEP:
            source = own[SHIFT + r]
        else:
            source = jnp.where(late[0] != 0, after_wrap[r - KEEP], after_main[r - KEEP])
        side[0, r, PAD:, :] = normed(source[:, :LANES], 0).T[:PAD]
        side[1, r, :PAD, :] = normed(source[:, tail:], 0).T[tile_cols - tail - PAD :]

    windows = ids.shape[2]
    own_last = spread_ids(ids, spread)[:, windows - 1 : windows]
    lane = lax.broadcasted_iota(jnp.int32, (KEYS, LANES), 1)
    digits = jnp.concatenate([left[2 * WIN + r].astype(F32) for r in range(WIN)], axis=0)
    halves = [digits[:, k : k + 1] + 256.0 * digits[:, k + 1 : k + 2] for k in range(0, 8, 2)]
    halves = [half.astype(jnp.int32) for half in halves]
    whole = [halves[2 * n + 1] * 65536 + halves[2 * n] for n in range(2)]
    spare = lax.broadcasted_iota(jnp.int32, (KEYS, LANES), 0) % PAD == WIN
    edge_b = jnp.where(spare, -1, jnp.broadcast_to(whole[0], (KEYS, LANES)))
    edge_a = jnp.where(spare, -1, jnp.where(lane == 0, whole[1], own_last))

    attend_row(tokens, att_b, windows, spread_ids(ids_before, spread), KEEP, SHIFT, wqkv, wproj, bias_b)
    skip = slice(PAD - KEEP, 2 * PAD - KEEP)
    window = [tokens[r, skip, :] for r in range(WIN)]
    branch = attend([window], edge_b, KEEP, SHIFT, wqkv, wproj, bias_b)
    for r in range(SHIFT):
        rim[0, r, skip, :] = branch[r * PAD : (r + 1) * PAD]
        rim[0, r, 2 * PAD - KEEP - 1 : 2 * PAD, :] = att_b[r, 2 * PAD - KEEP - 1 : 2 * PAD, :]
    pair = [[side[n, r, skip, :] for r in range(WIN)] for n in range(2)]
    branch = attend(pair, edge_a, 0, KEEP, wqkv, wproj, bias_a)
    for r in range(KEEP):
        low, high = r * PAD, (KEEP + r) * PAD
        rim[0, SHIFT + r, skip, :] = branch[low : low + PAD]
        rim[0, SHIFT + r, 2 * PAD - KEEP - 1 : 2 * PAD, :] = att_a[r, 2 * PAD - KEEP - 1 : 2 * PAD, :]
        rim[1, r, :PAD, :] = att_a[r, tile_cols : tile_cols + PAD, :]
        rim[1, r, skip, :] = branch[high : high + PAD]

    narrow = (0.5 * fc2[...].astype(F32)).astype(BF16)
    for r in range(tile_rows):
        if r < SHIFT:
            pieces = [rim[0, r, PAD:, :], att_b[r, 2 * PAD : PAD + tile_cols, :]]
        else:
            pieces = [rim[0, r, PAD:, :], att_a[r - SHIFT, 2 * PAD : tile_cols, :], rim[1, r - SHIFT, :PAD, :]]
        summed = own[r].astype(F32) + jnp.concatenate(pieces, axis=0).T
        second = layer_norm(summed, 0).astype(BF16)
        hidden = jnp.dot(fc1[...], second, preferred_element_type=F32)
        hidden = (hidden * (1.0 + lax.erf(hidden * (0.5**0.5)))).astype(BF16)
        out[r] = (summed + jnp.dot(narrow, hidden, preferred_element_type=F32)).astype(BF16)


def shards(features, region_ids, qkv_weight, proj_weight, rel_bias, fc1_weight, fc2_weight):
    tile_rows, tile_cols, width = features.shape
    tile = rowmajor(jnp.swapaxes(features, 1, 2))
    height = lax.axis_size("row")
    slide, row, col = lax.axis_index("slide"), lax.axis_index("row"), lax.axis_index("col")

    def in_wrap(s, r, c):
        return r == 0 or r == height - 1 or (s == 0 and r == 1 and c == 0)

    late = (row >= height - 2) | ((slide == 0) & (row == 0) & (col == 0))
    late = late.astype(jnp.int32).reshape(1)
    onehot = jnp.asarray(bias_onehot(), BF16)
    table = rel_bias.T
    tokens_first = functools.partial(jnp.transpose, axes=(2, 0, 1))
    ids = tokens_first(region_ids)
    att_shape = jax.ShapeDtypeStruct((KEEP, tile_cols + 2 * PAD, width), F32)
    scratch = [
        pltpu.VMEM((WIN, tile_cols + 2 * PAD, width), F32),
        pltpu.VMEM((width, 3 * LANES), BF16),
        pltpu.VMEM((HEADS, PAD, LANES), F32),
        pltpu.VMEM((KEYS, LANES), jnp.int32),
    ]

    def call(kernel, operands, out_shape, scratch_shapes):
        smem, vmem = pl.BlockSpec(memory_space=pltpu.SMEM), pl.BlockSpec(memory_space=pltpu.VMEM)
        return pl.pallas_call(
            kernel,
            out_shape=out_shape,
            in_specs=[smem] + [vmem] * (len(operands) - 1),
            out_specs=jax.tree.map(lambda _: vmem, out_shape),
            scratch_shapes=scratch_shapes,
            compiler_params=pltpu.CompilerParams(vmem_limit_bytes=20 * 1024 * 1024),
        )(*operands)

    before = rowmajor(moved(rowmajor(tile[SHIFT:]), 1, 0))
    ids_before = tokens_first(moved(region_ids, 1, 0))
    after_main = rowmajor(moved(rowmajor(tile[:SHIFT]), -1, 0, lambda s, r, c: not in_wrap(s, r, c)))
    weights = [qkv_weight, proj_weight, table, onehot]
    att = call(early_kernel, [late, tile, after_main, ids, *weights], att_shape, scratch)
    after_wrap = rowmajor(moved(rowmajor(tile[:SHIFT]), -1, 0, in_wrap))
    left, right = call(
        pack_kernel,
        [late, tile, before, after_main, after_wrap, ids, ids_before],
        (
            jax.ShapeDtypeStruct((3 * WIN, PAD, width), BF16),
            jax.ShapeDtypeStruct((2 * WIN, PAD, width), BF16),
        ),
        scratch[-1:],
    )
    left = moved(left, 0, 1)
    right = moved(right, 0, -1)
    att = call(late_kernel, [late, att, tile, after_wrap, ids, *weights], att_shape, scratch)
    result = call(
        final_kernel,
        [late, tile, before, after_main, after_wrap, left, right, ids, ids_before, *weights]
        + [fc1_weight.T, fc2_weight.T, att],
        jax.ShapeDtypeStruct((tile_rows, width, tile_cols), BF16),
        [
            *scratch,
            pltpu.VMEM((SHIFT, tile_cols + 2 * PAD, width), F32),
            pltpu.VMEM((2, WIN, 2 * PAD, width), F32),
            pltpu.VMEM((2, WIN, 2 * PAD, width), F32),
        ],
    )
    return jnp.swapaxes(result, 1, 2)


def solution(mesh):
    spec = P(("slide", "row"), "col", None)
    return jax.shard_map(
        shards,
        mesh=mesh,
        in_specs=(spec, spec, P(), P(), P(), P(), P()),
        out_specs=spec,
        check_vma=False,
    )
```

time: 89 us -> 81.3 us (0.913)
  local copies, waits for them, and re-layouts: 7.01 us -> 2.2 us
  waiting for transfers between devices: 1.52 us -> 5.06 us
  other arithmetic: 2.45 us -> 0 us
  matrix products: 2.44 us -> 0 us
  starting transfers between devices: 54.9 us -> 52.9 us
    ppermute x6, waiting for transfers between devices: 1.52 us -> 5.06 us  [moved(): return lax.ppermute(value, ('slide', 'row', 'col'), pairs)]
    slice x18 -> x1, local copies, waits for them, and re-layouts: 2.7 us -> 0.02 us  [shards(): tile[:SHIFT]]
    dot_general x1 -> x0, matrix products: 2.44 us -> none  [bias_of(): jnp.einsum('qpk,ph->hqk', chosen.astype(F32), rel_bias, precision=lax.Pre...]
    another operation x3 -> x0, other arithmetic: 2.05 us -> none
    ppermute x6, starting transfers between devices: 54.9 us -> 52.9 us  [moved(): return lax.ppermute(value, ('slide', 'row', 'col'), pairs)]
    another operation x15 -> x0, local copies, waits for them, and re-layouts: 1.18 us -> none  [the longest x10 0.94 us: rowmajor(): with_layout_constraint(value, Layout(major_to_minor=tuple(range(value.ndi...]
    pallas_call x3 -> x4, Pallas kernels: 19.9 us -> 20.6 us  [call(): pl.pallas_call(kernel, out_shape=out_shape, in_specs=[smem] + [vmem] * (l...]
  transfers between devices with their start and end apart: 6 -> 6, of which waited for: 1 -> 1; matrix products, arithmetic and copies ran while one was open for 12% -> 0% of each run, Pallas kernels for 11% -> 13%
where the time goes in v2:
time: 81.3 us; the launch traced here: 81 us
  starting transfers between devices  52.9 us (65%)
  Pallas kernels  20.6 us (25%)
  waiting for transfers between devices  5.06 us (6%)
  local copies, waits for them, and re-layouts  2.2 us (3%)
    ppermute x6, starting transfers between devices, moved(): return lax.ppermute(value, ('slide', 'row', 'col'), pairs)  52.9 us
    pallas_call x4, Pallas kernels, call(): pl.pallas_call(kernel, out_shape=out_shape, in_specs=[smem] + [vmem] * (l...  20.6 us
    ppermute x6, waiting for transfers between devices, moved(): return lax.ppermute(value, ('slide', 'row', 'col'), pairs)  5.06 us
  transfers between devices with their start and end apart: 6, of which 1 were waited for; matrix products, arithmetic and copies ran while one was open for 0% of the time, Pallas kernels for 13%

profile of v2, /device:TPU:40, one launch (start us, length us, event | category | flops | bytes accessed | tf_op | source)
XLA Modules:
  0.0 81.0 jit_solution(3174409911664629542)
XLA Ops:
  0.0 1.1 %slice.9 = bf16[4,96,448]{2,1,0:T(8,128)(2,1)S(1)} slice(bf16[7,96,448]{2,1,0:T(8,128)(2,1)} %bitcast.8), slice={[3:7], [0:96], [0:448]} | slice | bytes 688128 | tf_op jit(solution)/shard_map/slice | solution.py:322
  1.1 0.0 copy-start.3
  1.1 0.1 collective-permute-start
  1.2 0.0 copy-done
  1.2 1.3 %collective-permute-start.1 = (bf16[3,96,448]{2,1,0:T(8,128)(2,1)S(1)}, bf16[3,96,448]{2,1,0:T(8,128)(2,1)S(1)}, u32[]{:S(2)}, u32[]{:S(2)}) collective-permute-start(bf16[3,96,448]{2,1,0:T(8,128)(2,1)S(1)} %slice.10), channel_id=1, source_target_pairs={{5,1},{6,2},{7,3},{8,4},{9,5},{10,6},{11,7},{12,8},{13,9},{14,10},... | collective-permute-start | bytes 774152 | tf_op jit(solution)/shard_map/ppermute | solution.py:37
  2.6 44.2 %collective-permute-start.2 = (bf16[3,96,448]{2,1,0:T(8,128)(2,1)S(1)}, bf16[3,96,448]{2,1,0:T(8,128)(2,1)S(1)}, u32[]{:S(2)}, u32[]{:S(2)}) collective-permute-start(bf16[3,96,448]{2,1,0:T(8,128)(2,1)S(1)} %slice.10), channel_id=1, source_target_pairs={{0,252},{1,253},{2,254},{3,255},{4,0},{252,248},{253,249},{254,250... | collective-permute-start | bytes 774152 | tf_op jit(solution)/shard_map/ppermute | solution.py:37
  46.8 0.1 collective-permute-start.3
  46.9 5.0 %collective-permute-done.3 = s32[1,64,49]{1,0,2:T(1,128)S(1)} collective-permute-done((s32[1,64,49]{1,0,2:T(1,128)S(1)}, s32[1,64,49]{1,0,2:T(1,128)S(1)}, u32[]{:S(2)}, u32[]{:S(2)}) %collective-permute-start.3) | collective-permute-done | bytes 12576 | tf_op jit(solution)/shard_map/ppermute | solution.py:37
  51.9 0.0 collective-permute-done.1.after_main.refs_1_
  52.0 0.0 copy-start.7
  52.0 0.0 copy-start.1
  52.0 0.3 shard_map.82
  52.3 3.6 %collective-permute-start.4 = (bf16[21,8,96]{2,1,0:T(8,128)(2,1)S(1)}, bf16[21,8,96]{2,1,0:T(8,128)(2,1)S(1)}, u32[]{:S(2)}, u32[]{:S(2)}) collective-permute-start(bf16[21,8,96]{2,1,0:T(8,128)(2,1)S(1)} %get-tuple-element.7), channel_id=1, source_target_pairs={{0,1},{1,2},{2,3},{3,0},{4,5},{5,6},{6,7},{7,4},{8,9},{9,10},{10,1... | collective-permute-start | bytes 96776 | tf_op jit(solution)/shard_map/ppermute | solution.py:37
  55.9 0.0 copy-start.2
  55.9 0.0 copy-start.4
  55.9 3.7 %collective-permute-start.5 = (bf16[14,8,96]{2,1,0:T(8,128)(2,1)S(1)}, bf16[14,8,96]{2,1,0:T(8,128)(2,1)S(1)}, u32[]{:S(2)}, u32[]{:S(2)}) collective-permute-start(bf16[14,8,96]{2,1,0:T(8,128)(2,1)S(1)} %get-tuple-element.8), channel_id=1, source_target_pairs={{0,3},{1,0},{2,1},{3,2},{4,7},{5,4},{6,5},{7,6},{8,11},{9,8},{10,9... | collective-permute-start | bytes 64520 | tf_op jit(solution)/shard_map/ppermute | solution.py:37
  59.6 0.0 copy-start.6
  59.6 0.1 copy.9
  59.7 0.5 copy-done.6
  60.3 10.0 %shard_map.83.early = f32[4,464,96]{2,1,0:T(8,128)S(1)} custom-call(s32[1]{0:T(128)} %bitcast.late, bf16[7,96,448]{2,1,0:T(8,128)(2,1)S(1)} %bitcast.11, bf16[3,96,448]{2,1,0:T(8,128)(2,1)S(1)} %collective-permute-done.1.after_main.refs_1_, s32[49,1,64]{2,1,0:T(1,128)S(1)} %bitcast.15, bf16[96,288]{1,0:T(8,128)(2,1)S(1)} %copy-done.2, ...), custom_call_target="tpu_custom_call" | custom-call | tf_op jit(solution)/shard_map/pallas_call | solution.py:313
  70.2 0.0 copy-start.5
  70.3 0.5 shard_map.84.att_a
  70.8 0.4 copy-done.5
  71.1 9.9 %shard_map.85 = bf16[7,96,448]{2,1,0:T(8,128)(2,1)} custom-call(s32[1]{0:T(128)} %bitcast.late, bf16[7,96,448]{2,1,0:T(8,128)(2,1)S(1)} %bitcast.13, bf16[4,96,448]{2,1,0:T(8,128)(2,1)S(1)} %collective-permute-done.before, bf16[3,96,448]{2,1,0:T(8,128)(2,1)S(1)} %collective-permute-done.1.after_main.refs_1_, ...), custom_call_target="tpu_custom_call" | custom-call | tf_op jit(solution)/shard_map/pallas_call | solution.py:313
  (11 shorter events, 0.0 us)
Async XLA Ops:
  0.0 1.2 %copy-start = (bf16[7,448,96]{1,2,0:T(8,128)(2,1)S(1)}, bf16[7,448,96]{1,2,0:T(8,128)(2,1)}, u32[]{:S(2)}) copy-start(bf16[7,448,96]{1,2,0:T(8,128)(2,1)} %param.8) | copy-start | bytes 1806340
  1.1 45.7 %copy-start.3 = (s32[1,64,49]{1,0,2:T(1,128)S(1)}, s32[1,64,49]{1,0,2:T(1,128)}, u32[]{:S(2)}) copy-start(s32[1,64,49]{1,0,2:T(1,128)} %param.9) | copy-start | bytes 37636
  1.1 50.8 %collective-permute-start = (bf16[4,96,448]{2,1,0:T(8,128)(2,1)S(1)}, bf16[4,96,448]{2,1,0:T(8,128)(2,1)S(1)}, u32[]{:S(2)}, u32[]{:S(2)}) collective-permute-start(bf16[4,96,448]{2,1,0:T(8,128)(2,1)S(1)} %slice.9), channel_id=1, source_target_pairs={{0,4},{1,5},{2,6},{3,7},{4,8},{5,9},{6,10},{7,11},{8,12},{9,13},{1... | collective-permute-start | bytes 1032200 | tf_op jit(solution)/shard_map/ppermute | solution.py:37
  1.2 50.7 %collective-permute-start.1 = (bf16[3,96,448]{2,1,0:T(8,128)(2,1)S(1)}, bf16[3,96,448]{2,1,0:T(8,128)(2,1)S(1)}, u32[]{:S(2)}, u32[]{:S(2)}) collective-permute-start(bf16[3,96,448]{2,1,0:T(8,128)(2,1)S(1)} %slice.10), channel_id=1, source_target_pairs={{5,1},{6,2},{7,3},{8,4},{9,5},{10,6},{11,7},{12,8},{13,9},{14,10},... | collective-permute-start | bytes 774152 | tf_op jit(solution)/shard_map/ppermute | solution.py:37
  2.6 49.4 %collective-permute-start.2 = (bf16[3,96,448]{2,1,0:T(8,128)(2,1)S(1)}, bf16[3,96,448]{2,1,0:T(8,128)(2,1)S(1)}, u32[]{:S(2)}, u32[]{:S(2)}) collective-permute-start(bf16[3,96,448]{2,1,0:T(8,128)(2,1)S(1)} %slice.10), channel_id=1, source_target_pairs={{0,252},{1,253},{2,254},{3,255},{4,0},{252,248},{253,249},{254,250... | collective-permute-start | bytes 774152 | tf_op jit(solution)/shard_map/ppermute | solution.py:37
  46.8 5.1 %collective-permute-start.3 = (s32[1,64,49]{1,0,2:T(1,128)S(1)}, s32[1,64,49]{1,0,2:T(1,128)S(1)}, u32[]{:S(2)}, u32[]{:S(2)}) collective-permute-start(s32[1,64,49]{1,0,2:T(1,128)S(1)} %copy-done.3), channel_id=1, source_target_pairs={{0,4},{1,5},{2,6},{3,7},{4,8},{5,9},{6,10},{7,11},{8,12},{9,13},{1... | collective-permute-start | bytes 37640 | tf_op jit(solution)/shard_map/ppermute | solution.py:37
  52.0 7.6 %copy-start.7 = (bf16[96,384]{1,0:T(8,128)(2,1)S(1)}, bf16[96,384]{1,0:T(8,128)(2,1)}, u32[]{:S(2)}) copy-start(bf16[96,384]{1,0:T(8,128)(2,1)} %param.13) | copy-start | bytes 221188
  52.0 7.8 %copy-start.1 = (bf16[169,1024]{1,0:T(8,128)(2,1)S(1)}, bf16[169,1024]{1,0:T(8,128)(2,1)}, u32[]{:S(2)}) copy-start(bf16[169,1024]{1,0:T(8,128)(2,1)} %constant.21.clone.refs_6_.onehot) | copy-start | bytes 1038340
  52.3 18.5 %collective-permute-start.4 = (bf16[21,8,96]{2,1,0:T(8,128)(2,1)S(1)}, bf16[21,8,96]{2,1,0:T(8,128)(2,1)S(1)}, u32[]{:S(2)}, u32[]{:S(2)}) collective-permute-start(bf16[21,8,96]{2,1,0:T(8,128)(2,1)S(1)} %get-tuple-element.7), channel_id=1, source_target_pairs={{0,1},{1,2},{2,3},{3,0},{4,5},{5,6},{6,7},{7,4},{8,9},{9,10},{10,1... | collective-permute-start | bytes 96776 | tf_op jit(solution)/shard_map/ppermute | solution.py:37
  55.9 3.9 %copy-start.2 = (bf16[96,288]{1,0:T(8,128)(2,1)S(1)}, bf16[96,288]{1,0:T(8,128)(2,1)}, u32[]{:S(2)}) copy-start(bf16[96,288]{1,0:T(8,128)(2,1)} %weight.1) | copy-start | bytes 165892
  55.9 3.9 %copy-start.4 = (bf16[96,96]{1,0:T(8,128)(2,1)S(1)}, bf16[96,96]{1,0:T(8,128)(2,1)}, u32[]{:S(2)}) copy-start(bf16[96,96]{1,0:T(8,128)(2,1)} %wproj.1) | copy-start | bytes 55300
  55.9 14.9 %collective-permute-start.5 = (bf16[14,8,96]{2,1,0:T(8,128)(2,1)S(1)}, bf16[14,8,96]{2,1,0:T(8,128)(2,1)S(1)}, u32[]{:S(2)}, u32[]{:S(2)}) collective-permute-start(bf16[14,8,96]{2,1,0:T(8,128)(2,1)S(1)} %get-tuple-element.8), channel_id=1, source_target_pairs={{0,3},{1,0},{2,1},{3,2},{4,7},{5,4},{6,5},{7,6},{8,11},{9,8},{10,9... | collective-permute-start | bytes 64520 | tf_op jit(solution)/shard_map/ppermute | solution.py:37
  59.6 0.7 copy-start.6
  70.2 0.9 %copy-start.5 = (bf16[384,96]{0,1:T(8,128)(2,1)S(1)}, bf16[384,96]{0,1:T(8,128)(2,1)}, u32[]{:S(2)}) copy-start(bf16[384,96]{0,1:T(8,128)(2,1)} %param.14) | copy-start | bytes 221188

commit v3 on v2

--- a/solution.py
+++ b/solution.py
@@ -196,6 +196,18 @@
         left[2 * WIN + r] = digits[r * PAD : (r + 1) * PAD].astype(BF16)
 
 
+def upper_kernel(late, own, before, ids_before, weight, wproj, rel_bias, onehot, att, tokens, wqkv, strip, spread):
+    tile_cols = own.shape[2]
+    widen(weight, wqkv)
+    fill_strip(rel_bias, onehot, strip)
+    for r in range(WIN):
+        source = before[r] if r < KEEP else own[r - KEEP]
+        tokens[r, PAD : PAD + tile_cols, :] = normed(source, 0).T
+    bias = bias_tiles(strip, KEEP, SHIFT)
+    count = tile_cols // WIN - 1
+    attend_row(tokens, att, count, spread_ids(ids_before, spread), KEEP, SHIFT, wqkv, wproj, bias)
+
+
 def final_kernel(
     late,
     own,
@@ -213,12 +225,11 @@
     fc1,
     fc2,
     att_a,
+    att_b,
     out,
-    tokens,
     wqkv,
     strip,
     spread,
-    att_b,
     side,
     rim,
 ):
@@ -227,57 +238,47 @@
     fill_strip(rel_bias, onehot, strip)
     bias_a = bias_tiles(strip, 0, KEEP)
     bias_b = bias_tiles(strip, KEEP, SHIFT)
-    for r in range(WIN):
-        source = before[r] if r < KEEP else own[r - KEEP]
-        tokens[r, PAD : PAD + tile_cols, :] = normed(source, 0).T
     halo_left = normed(left[: 2 * WIN], -1)
     halo_right = normed(right[...], -1)
-    tokens[:, :PAD, :] = halo_left[:WIN]
-    tokens[:, PAD + tile_cols :, :] = halo_right[:WIN]
-    side[0, :, :PAD, :] = halo_left[WIN:]
-    side[1, :, PAD:, :] = halo_right[WIN:]
     tail = tile_cols // LANES * LANES
-    for r in range(WIN):
+    for r in range(2 * WIN):
         if r < KEEP:
-            source = own[SHIFT + r]
+            source = before[r]
+        elif r < KEEP + WIN:
+            source = own[r - KEEP]
         else:
-            source = jnp.where(late[0] != 0, after_wrap[r - KEEP], after_main[r - KEEP])
+            source = jnp.where(late[0] != 0, after_wrap[r - KEEP - WIN], after_main[r - KEEP - WIN])
+        side[0, r, :PAD, :] = halo_left[r]
         side[0, r, PAD:, :] = normed(source[:, :LANES], 0).T[:PAD]
         side[1, r, :PAD, :] = normed(source[:, tail:], 0).T[tile_cols - tail - PAD :]
+        side[1, r, PAD:, :] = halo_right[r]
 
     windows = ids.shape[2]
-    own_last = spread_ids(ids, spread)[:, windows - 1 : windows]
+    lasts = [spread_ids(each, spread)[:, windows - 1 : windows] for each in (ids_before, ids)]
     lane = lax.broadcasted_iota(jnp.int32, (KEYS, LANES), 1)
     digits = jnp.concatenate([left[2 * WIN + r].astype(F32) for r in range(WIN)], axis=0)
     halves = [digits[:, k : k + 1] + 256.0 * digits[:, k + 1 : k + 2] for k in range(0, 8, 2)]
     halves = [half.astype(jnp.int32) for half in halves]
     whole = [halves[2 * n + 1] * 65536 + halves[2 * n] for n in range(2)]
     spare = lax.broadcasted_iota(jnp.int32, (KEYS, LANES), 0) % PAD == WIN
-    edge_b = jnp.where(spare, -1, jnp.broadcast_to(whole[0], (KEYS, LANES)))
-    edge_a = jnp.where(spare, -1, jnp.where(lane == 0, whole[1], own_last))
-
-    attend_row(tokens, att_b, windows, spread_ids(ids_before, spread), KEEP, SHIFT, wqkv, wproj, bias_b)
+    edge_ids = [jnp.where(spare, -1, jnp.where(lane == 0, whole[n], lasts[n])) for n in range(2)]
+
     skip = slice(PAD - KEEP, 2 * PAD - KEEP)
-    window = [tokens[r, skip, :] for r in range(WIN)]
-    branch = attend([window], edge_b, KEEP, SHIFT, wqkv, wproj, bias_b)
-    for r in range(SHIFT):
-        rim[0, r, skip, :] = branch[r * PAD : (r + 1) * PAD]
-        rim[0, r, 2 * PAD - KEEP - 1 : 2 * PAD, :] = att_b[r, 2 * PAD - KEEP - 1 : 2 * PAD, :]
-    pair = [[side[n, r, skip, :] for r in range(WIN)] for n in range(2)]
-    branch = attend(pair, edge_a, 0, KEEP, wqkv, wproj, bias_a)
-    for r in range(KEEP):
-        low, high = r * PAD, (KEEP + r) * PAD
-        rim[0, SHIFT + r, skip, :] = branch[low : low + PAD]
-        rim[0, SHIFT + r, 2 * PAD - KEEP - 1 : 2 * PAD, :] = att_a[r, 2 * PAD - KEEP - 1 : 2 * PAD, :]
-        rim[1, r, :PAD, :] = att_a[r, tile_cols : tile_cols + PAD, :]
-        rim[1, r, skip, :] = branch[high : high + PAD]
+    rest = slice(2 * PAD - KEEP - 1, 2 * PAD)
+    for n, (first, rows, bias, att) in enumerate(((KEEP, SHIFT, bias_b, att_b), (0, KEEP, bias_a, att_a))):
+        pair = [[side[m, n * WIN + r, skip, :] for r in range(WIN)] for m in range(2)]
+        branch = attend(pair, edge_ids[n], first, rows, wqkv, wproj, bias)
+        for r in range(rows):
+            low, high, place = r * PAD, (rows + r) * PAD, n * SHIFT + r
+            rim[0, place, skip, :] = branch[low : low + PAD]
+            rim[0, place, rest, :] = att[r, rest, :]
+            rim[1, place, :PAD, :] = att[r, tile_cols : tile_cols + PAD, :]
+            rim[1, place, skip, :] = branch[high : high + PAD]
 
     narrow = (0.5 * fc2[...].astype(F32)).astype(BF16)
     for r in range(tile_rows):
-        if r < SHIFT:
-            pieces = [rim[0, r, PAD:, :], att_b[r, 2 * PAD : PAD + tile_cols, :]]
-        else:
-            pieces = [rim[0, r, PAD:, :], att_a[r - SHIFT, 2 * PAD : tile_cols, :], rim[1, r - SHIFT, :PAD, :]]
+        inner = att_b[r, 2 * PAD : tile_cols, :] if r < SHIFT else att_a[r - SHIFT, 2 * PAD : tile_cols, :]
+        pieces = [rim[0, r, PAD:, :], inner, rim[1, r, :PAD, :]]
         summed = own[r].astype(F32) + jnp.concatenate(pieces, axis=0).T
         second = layer_norm(summed, 0).astype(BF16)
         hidden = jnp.dot(fc1[...], second, preferred_element_type=F32)
@@ -337,17 +338,14 @@
     left = moved(left, 0, 1)
     right = moved(right, 0, -1)
     att = call(late_kernel, [late, att, tile, after_wrap, ids, *weights], att_shape, scratch)
+    upper = jax.ShapeDtypeStruct((SHIFT, tile_cols + 2 * PAD, width), F32)
+    att_b = call(upper_kernel, [late, tile, before, ids_before, *weights], upper, scratch)
     result = call(
         final_kernel,
         [late, tile, before, after_main, after_wrap, left, right, ids, ids_before, *weights]
-        + [fc1_weight.T, fc2_weight.T, att],
+        + [fc1_weight.T, fc2_weight.T, att, att_b],
         jax.ShapeDtypeStruct((tile_rows, width, tile_cols), BF16),
-        [
-            *scratch,
-            pltpu.VMEM((SHIFT, tile_cols + 2 * PAD, width), F32),
-            pltpu.VMEM((2, WIN, 2 * PAD, width), F32),
-            pltpu.VMEM((2, WIN, 2 * PAD, width), F32),
-        ],
+        [*scratch[1:], pltpu.VMEM((2, 2 * WIN, 2 * PAD, width), F32), pltpu.VMEM((2, WIN, 2 * PAD, width), F32)],
     )
     return jnp.swapaxes(result, 1, 2)
 

time: 81.3 us -> 81.7 us (level)
    pallas_call x4 -> x5, Pallas kernels: 20.6 us -> 21.3 us  [call(): pl.pallas_call(kernel, out_shape=out_shape, in_specs=[smem] + [vmem] * (l...]
  transfers between devices with their start and end apart: 6 -> 6, of which waited for: 1 -> 1; matrix products, arithmetic and copies ran while one was open for 0% -> 0% of each run, Pallas kernels for 13% -> 20%
where the time goes in v3:
time: 81.7 us; the launch traced here: 81.4 us
  starting transfers between devices  52.9 us (65%)
  Pallas kernels  21.3 us (26%)
  waiting for transfers between devices  5.06 us (6%)
  local copies, waits for them, and re-layouts  1.83 us (2%)
    ppermute x6, starting transfers between devices, moved(): return lax.ppermute(value, ('slide', 'row', 'col'), pairs)  52.9 us
    pallas_call x5, Pallas kernels, call(): pl.pallas_call(kernel, out_shape=out_shape, in_specs=[smem] + [vmem] * (l...  21.3 us
    ppermute x6, waiting for transfers between devices, moved(): return lax.ppermute(value, ('slide', 'row', 'col'), pairs)  5.06 us
  transfers between devices with their start and end apart: 6, of which 1 were waited for; matrix products, arithmetic and copies ran while one was open for 0% of the time, Pallas kernels for 20%

profile of v3, /device:TPU:40, one launch (start us, length us, event | category | flops | bytes accessed | tf_op | source)
XLA Modules:
  0.0 81.4 jit_solution(2652559533809143368)
XLA Ops:
  0.0 1.1 %slice.9 = bf16[4,96,448]{2,1,0:T(8,128)(2,1)S(1)} slice(bf16[7,96,448]{2,1,0:T(8,128)(2,1)} %bitcast.8), slice={[3:7], [0:96], [0:448]} | slice | bytes 688128 | tf_op jit(solution)/shard_map/slice | solution.py:323
  1.1 0.0 copy-start.3
  1.1 0.1 collective-permute-start
  1.2 0.0 copy-done
  1.2 1.3 %collective-permute-start.1 = (bf16[3,96,448]{2,1,0:T(8,128)(2,1)S(1)}, bf16[3,96,448]{2,1,0:T(8,128)(2,1)S(1)}, u32[]{:S(2)}, u32[]{:S(2)}) collective-permute-start(bf16[3,96,448]{2,1,0:T(8,128)(2,1)S(1)} %slice.10), channel_id=1, source_target_pairs={{5,1},{6,2},{7,3},{8,4},{9,5},{10,6},{11,7},{12,8},{13,9},{14,10},... | collective-permute-start | bytes 774152 | tf_op jit(solution)/shard_map/ppermute | solution.py:37
  2.6 44.2 %collective-permute-start.2 = (bf16[3,96,448]{2,1,0:T(8,128)(2,1)S(1)}, bf16[3,96,448]{2,1,0:T(8,128)(2,1)S(1)}, u32[]{:S(2)}, u32[]{:S(2)}) collective-permute-start(bf16[3,96,448]{2,1,0:T(8,128)(2,1)S(1)} %slice.10), channel_id=1, source_target_pairs={{0,252},{1,253},{2,254},{3,255},{4,0},{252,248},{253,249},{254,250... | collective-permute-start | bytes 774152 | tf_op jit(solution)/shard_map/ppermute | solution.py:37
  46.8 0.1 collective-permute-start.3
  46.9 5.0 %collective-permute-done.3 = s32[1,64,49]{1,0,2:T(1,128)S(1)} collective-permute-done((s32[1,64,49]{1,0,2:T(1,128)S(1)}, s32[1,64,49]{1,0,2:T(1,128)S(1)}, u32[]{:S(2)}, u32[]{:S(2)}) %collective-permute-start.3) | collective-permute-done | bytes 12576 | tf_op jit(solution)/shard_map/ppermute | solution.py:37
  52.0 0.0 copy-start.7
  52.0 0.0 copy-start.1
  52.0 0.3 shard_map.82
  52.3 3.6 %collective-permute-start.4 = (bf16[21,8,96]{2,1,0:T(8,128)(2,1)S(1)}, bf16[21,8,96]{2,1,0:T(8,128)(2,1)S(1)}, u32[]{:S(2)}, u32[]{:S(2)}) collective-permute-start(bf16[21,8,96]{2,1,0:T(8,128)(2,1)S(1)} %get-tuple-element.7), channel_id=1, source_target_pairs={{0,1},{1,2},{2,3},{3,0},{4,5},{5,6},{6,7},{7,4},{8,9},{9,10},{10,1... | collective-permute-start | bytes 96776 | tf_op jit(solution)/shard_map/ppermute | solution.py:37
  55.9 0.0 copy-start.2
  55.9 0.0 copy-start.4
  55.9 3.7 %collective-permute-start.5 = (bf16[14,8,96]{2,1,0:T(8,128)(2,1)S(1)}, bf16[14,8,96]{2,1,0:T(8,128)(2,1)S(1)}, u32[]{:S(2)}, u32[]{:S(2)}) collective-permute-start(bf16[14,8,96]{2,1,0:T(8,128)(2,1)S(1)} %get-tuple-element.8), channel_id=1, source_target_pairs={{0,3},{1,0},{2,1},{3,2},{4,7},{5,4},{6,5},{7,6},{8,11},{9,8},{10,9... | collective-permute-start | bytes 64520 | tf_op jit(solution)/shard_map/ppermute | solution.py:37
  59.6 0.0 copy-start.6
  59.6 0.1 copy.9
  59.7 0.5 copy-done.6
  60.3 10.0 %shard_map.83.early = f32[4,464,96]{2,1,0:T(8,128)S(1)} custom-call(s32[1]{0:T(128)} %bitcast.late, bf16[7,96,448]{2,1,0:T(8,128)(2,1)S(1)} %bitcast.11, bf16[3,96,448]{2,1,0:T(8,128)(2,1)S(1)} %collective-permute-done.1.after_main.refs_1_, s32[49,1,64]{2,1,0:T(1,128)S(1)} %bitcast.16, bf16[96,288]{1,0:T(8,128)(2,1)S(1)} %copy-done.2, ...), custom_call_target="tpu_custom_call" | custom-call | tf_op jit(solution)/shard_map/pallas_call | solution.py:314
  70.2 0.5 shard_map.84.att_a
  70.7 0.0 copy-start.5
  70.7 5.9 %shard_map.85.att_b = f32[3,464,96]{2,1,0:T(8,128)S(1)} custom-call(s32[1]{0:T(128)} %bitcast.late, bf16[7,96,448]{2,1,0:T(8,128)(2,1)S(1)} %bitcast.13, bf16[4,96,448]{2,1,0:T(8,128)(2,1)S(1)} %collective-permute-done.before, s32[49,1,64]{2,1,0:T(1,128)S(1)} %bitcast.21, bf16[96,288]{1,0:T(8,128)(2,1)S(1)} %copy-done.2, bf16[96,96]{1,0:T(8,128)(2,1)S(1)} %copy-done.4, ...), custom_call_target="tpu_custom_call" | custom-call | tf_op jit(solution)/shard_map/pallas_call | solution.py:314
  76.7 0.0 collective-permute-done.4.left
  76.7 4.7 %shard_map.86 = bf16[7,96,448]{2,1,0:T(8,128)(2,1)} custom-call(s32[1]{0:T(128)} %bitcast.late, bf16[7,96,448]{2,1,0:T(8,128)(2,1)S(1)} %bitcast.14, bf16[4,96,448]{2,1,0:T(8,128)(2,1)S(1)} %collective-permute-done.before, bf16[3,96,448]{2,1,0:T(8,128)(2,1)S(1)} %collective-permute-done.1.after_main.refs_1_, ...), custom_call_target="tpu_custom_call" | custom-call | tf_op jit(solution)/shard_map/pallas_call | solution.py:314
  (12 shorter events, 0.0 us)
Async XLA Ops:
  0.0 1.2 %copy-start = (bf16[7,448,96]{1,2,0:T(8,128)(2,1)S(1)}, bf16[7,448,96]{1,2,0:T(8,128)(2,1)}, u32[]{:S(2)}) copy-start(bf16[7,448,96]{1,2,0:T(8,128)(2,1)} %param.8) | copy-start | bytes 1806340
  1.1 45.7 %copy-start.3 = (s32[1,64,49]{1,0,2:T(1,128)S(1)}, s32[1,64,49]{1,0,2:T(1,128)}, u32[]{:S(2)}) copy-start(s32[1,64,49]{1,0,2:T(1,128)} %param.9) | copy-start | bytes 37636
  1.1 50.8 %collective-permute-start = (bf16[4,96,448]{2,1,0:T(8,128)(2,1)S(1)}, bf16[4,96,448]{2,1,0:T(8,128)(2,1)S(1)}, u32[]{:S(2)}, u32[]{:S(2)}) collective-permute-start(bf16[4,96,448]{2,1,0:T(8,128)(2,1)S(1)} %slice.9), channel_id=1, source_target_pairs={{0,4},{1,5},{2,6},{3,7},{4,8},{5,9},{6,10},{7,11},{8,12},{9,13},{1... | collective-permute-start | bytes 1032200 | tf_op jit(solution)/shard_map/ppermute | solution.py:37
  1.2 50.7 %collective-permute-start.1 = (bf16[3,96,448]{2,1,0:T(8,128)(2,1)S(1)}, bf16[3,96,448]{2,1,0:T(8,128)(2,1)S(1)}, u32[]{:S(2)}, u32[]{:S(2)}) collective-permute-start(bf16[3,96,448]{2,1,0:T(8,128)(2,1)S(1)} %slice.10), channel_id=1, source_target_pairs={{5,1},{6,2},{7,3},{8,4},{9,5},{10,6},{11,7},{12,8},{13,9},{14,10},... | collective-permute-start | bytes 774152 | tf_op jit(solution)/shard_map/ppermute | solution.py:37
  2.6 49.4 %collective-permute-start.2 = (bf16[3,96,448]{2,1,0:T(8,128)(2,1)S(1)}, bf16[3,96,448]{2,1,0:T(8,128)(2,1)S(1)}, u32[]{:S(2)}, u32[]{:S(2)}) collective-permute-start(bf16[3,96,448]{2,1,0:T(8,128)(2,1)S(1)} %slice.10), channel_id=1, source_target_pairs={{0,252},{1,253},{2,254},{3,255},{4,0},{252,248},{253,249},{254,250... | collective-permute-start | bytes 774152 | tf_op jit(solution)/shard_map/ppermute | solution.py:37
  46.8 5.1 %collective-permute-start.3 = (s32[1,64,49]{1,0,2:T(1,128)S(1)}, s32[1,64,49]{1,0,2:T(1,128)S(1)}, u32[]{:S(2)}, u32[]{:S(2)}) collective-permute-start(s32[1,64,49]{1,0,2:T(1,128)S(1)} %copy-done.3), channel_id=1, source_target_pairs={{0,4},{1,5},{2,6},{3,7},{4,8},{5,9},{6,10},{7,11},{8,12},{9,13},{1... | collective-permute-start | bytes 37640 | tf_op jit(solution)/shard_map/ppermute | solution.py:37
  52.0 7.6 %copy-start.7 = (bf16[96,384]{1,0:T(8,128)(2,1)S(1)}, bf16[96,384]{1,0:T(8,128)(2,1)}, u32[]{:S(2)}) copy-start(bf16[96,384]{1,0:T(8,128)(2,1)} %param.13) | copy-start | bytes 221188
  52.0 7.8 %copy-start.1 = (bf16[169,1024]{1,0:T(8,128)(2,1)S(1)}, bf16[169,1024]{1,0:T(8,128)(2,1)}, u32[]{:S(2)}) copy-start(bf16[169,1024]{1,0:T(8,128)(2,1)} %constant.21.clone.refs_6_.onehot) | copy-start | bytes 1038340
  52.3 24.4 %collective-permute-start.4 = (bf16[21,8,96]{2,1,0:T(8,128)(2,1)S(1)}, bf16[21,8,96]{2,1,0:T(8,128)(2,1)S(1)}, u32[]{:S(2)}, u32[]{:S(2)}) collective-permute-start(bf16[21,8,96]{2,1,0:T(8,128)(2,1)S(1)} %get-tuple-element.7), channel_id=1, source_target_pairs={{0,1},{1,2},{2,3},{3,0},{4,5},{5,6},{6,7},{7,4},{8,9},{9,10},{10,1... | collective-permute-start | bytes 96776 | tf_op jit(solution)/shard_map/ppermute | solution.py:37
  55.9 3.9 %copy-start.2 = (bf16[96,288]{1,0:T(8,128)(2,1)S(1)}, bf16[96,288]{1,0:T(8,128)(2,1)}, u32[]{:S(2)}) copy-start(bf16[96,288]{1,0:T(8,128)(2,1)} %weight.3) | copy-start | bytes 165892
  55.9 3.9 %copy-start.4 = (bf16[96,96]{1,0:T(8,128)(2,1)S(1)}, bf16[96,96]{1,0:T(8,128)(2,1)}, u32[]{:S(2)}) copy-start(bf16[96,96]{1,0:T(8,128)(2,1)} %wproj.3) | copy-start | bytes 55300
  55.9 20.8 %collective-permute-start.5 = (bf16[14,8,96]{2,1,0:T(8,128)(2,1)S(1)}, bf16[14,8,96]{2,1,0:T(8,128)(2,1)S(1)}, u32[]{:S(2)}, u32[]{:S(2)}) collective-permute-start(bf16[14,8,96]{2,1,0:T(8,128)(2,1)S(1)} %get-tuple-element.8), channel_id=1, source_target_pairs={{0,3},{1,0},{2,1},{3,2},{4,7},{5,4},{6,5},{7,6},{8,11},{9,8},{10,9... | collective-permute-start | bytes 64520 | tf_op jit(solution)/shard_map/ppermute | solution.py:37
  59.6 0.7 copy-start.6
  70.7 6.0 %copy-start.5 = (bf16[384,96]{0,1:T(8,128)(2,1)S(1)}, bf16[384,96]{0,1:T(8,128)(2,1)}, u32[]{:S(2)}) copy-start(bf16[384,96]{0,1:T(8,128)(2,1)} %param.14) | copy-start | bytes 221188

commit v4 on v3

--- a/solution.py
+++ b/solution.py
@@ -16,7 +16,7 @@
 KEEP = WIN - SHIFT
 PAD = 8
 KEYS = WIN * PAD
-GROUP = 13
+GROUP = 16
 LANES = 128
 NEG = -1e30
 F32 = jnp.float32
@@ -165,11 +165,7 @@
         lower_windows(*refs)
 
 
-def late_kernel(late, early, *refs):
-    @pl.when(late[0] == 0)
-    def _():
-        refs[7][...] = early[...]
-
+def late_kernel(late, *refs):
     @pl.when(late[0] != 0)
     def _():
         lower_windows(*refs)
@@ -224,7 +220,8 @@
     onehot,
     fc1,
     fc2,
-    att_a,
+    att_early,
+    att_late,
     att_b,
     out,
     wqkv,
@@ -263,21 +260,28 @@
     spare = lax.broadcasted_iota(jnp.int32, (KEYS, LANES), 0) % PAD == WIN
     edge_ids = [jnp.where(spare, -1, jnp.where(lane == 0, whole[n], lasts[n])) for n in range(2)]
 
+    def att_a(r, part):
+        return jnp.where(late[0] != 0, att_late[r, part, :], att_early[r, part, :])
+
+    def att_upper(r, part):
+        return att_b[r, part, :]
+
     skip = slice(PAD - KEEP, 2 * PAD - KEEP)
     rest = slice(2 * PAD - KEEP - 1, 2 * PAD)
-    for n, (first, rows, bias, att) in enumerate(((KEEP, SHIFT, bias_b, att_b), (0, KEEP, bias_a, att_a))):
+    for n, (first, rows, bias, att) in enumerate(((KEEP, SHIFT, bias_b, att_upper), (0, KEEP, bias_a, att_a))):
         pair = [[side[m, n * WIN + r, skip, :] for r in range(WIN)] for m in range(2)]
         branch = attend(pair, edge_ids[n], first, rows, wqkv, wproj, bias)
         for r in range(rows):
             low, high, place = r * PAD, (rows + r) * PAD, n * SHIFT + r
             rim[0, place, skip, :] = branch[low : low + PAD]
-            rim[0, place, rest, :] = att[r, rest, :]
-            rim[1, place, :PAD, :] = att[r, tile_cols : tile_cols + PAD, :]
+            rim[0, place, rest, :] = att(r, rest)
+            rim[1, place, :PAD, :] = att(r, slice(tile_cols, tile_cols + PAD))
             rim[1, place, skip, :] = branch[high : high + PAD]
 
     narrow = (0.5 * fc2[...].astype(F32)).astype(BF16)
     for r in range(tile_rows):
-        inner = att_b[r, 2 * PAD : tile_cols, :] if r < SHIFT else att_a[r - SHIFT, 2 * PAD : tile_cols, :]
+        middle = slice(2 * PAD, tile_cols)
+        inner = att_upper(r, middle) if r < SHIFT else att_a(r - SHIFT, middle)
         pieces = [rim[0, r, PAD:, :], inner, rim[1, r, :PAD, :]]
         summed = own[r].astype(F32) + jnp.concatenate(pieces, axis=0).T
         second = layer_norm(summed, 0).astype(BF16)
@@ -337,13 +341,13 @@
     )
     left = moved(left, 0, 1)
     right = moved(right, 0, -1)
-    att = call(late_kernel, [late, att, tile, after_wrap, ids, *weights], att_shape, scratch)
+    late_att = call(late_kernel, [late, tile, after_wrap, ids, *weights], att_shape, scratch)
     upper = jax.ShapeDtypeStruct((SHIFT, tile_cols + 2 * PAD, width), F32)
     att_b = call(upper_kernel, [late, tile, before, ids_before, *weights], upper, scratch)
     result = call(
         final_kernel,
         [late, tile, before, after_main, after_wrap, left, right, ids, ids_before, *weights]
-        + [fc1_weight.T, fc2_weight.T, att, att_b],
+        + [fc1_weight.T, fc2_weight.T, att, late_att, att_b],
         jax.ShapeDtypeStruct((tile_rows, width, tile_cols), BF16),
         [*scratch[1:], pltpu.VMEM((2, 2 * WIN, 2 * PAD, width), F32), pltpu.VMEM((2, WIN, 2 * PAD, width), F32)],
     )

time: 81.7 us -> 81.6 us (level)
  no operation moved by 1% of the time
where the time goes in v4:
time: 81.6 us; the launch traced here: 81.3 us
  starting transfers between devices  52.9 us (65%)
  Pallas kernels  21.3 us (26%)
  waiting for transfers between devices  5.07 us (6%)
  local copies, waits for them, and re-layouts  1.83 us (2%)
    ppermute x6, starting transfers between devices, moved(): return lax.ppermute(value, ('slide', 'row', 'col'), pairs)  52.9 us
    pallas_call x5, Pallas kernels, call(): pl.pallas_call(kernel, out_shape=out_shape, in_specs=[smem] + [vmem] * (l...  21.3 us
    ppermute x6, waiting for transfers between devices, moved(): return lax.ppermute(value, ('slide', 'row', 'col'), pairs)  5.07 us
  transfers between devices with their start and end apart: 6, of which 1 were waited for; matrix products, arithmetic and copies ran while one was open for 0% of the time, Pallas kernels for 20%

profile of v4, /device:TPU:40, one launch (start us, length us, event | category | flops | bytes accessed | tf_op | source)
XLA Modules:
  0.0 81.3 jit_solution(11519025685527054354)
XLA Ops:
  0.0 1.1 %slice.9 = bf16[4,96,448]{2,1,0:T(8,128)(2,1)S(1)} slice(bf16[7,96,448]{2,1,0:T(8,128)(2,1)} %bitcast.8), slice={[3:7], [0:96], [0:448]} | slice | bytes 688128 | tf_op jit(solution)/shard_map/slice | solution.py:327
  1.1 0.0 copy-start.3
  1.1 0.1 collective-permute-start
  1.2 0.0 copy-done
  1.2 1.3 %collective-permute-start.1 = (bf16[3,96,448]{2,1,0:T(8,128)(2,1)S(1)}, bf16[3,96,448]{2,1,0:T(8,128)(2,1)S(1)}, u32[]{:S(2)}, u32[]{:S(2)}) collective-permute-start(bf16[3,96,448]{2,1,0:T(8,128)(2,1)S(1)} %slice.10), channel_id=1, source_target_pairs={{5,1},{6,2},{7,3},{8,4},{9,5},{10,6},{11,7},{12,8},{13,9},{14,10},... | collective-permute-start | bytes 774152 | tf_op jit(solution)/shard_map/ppermute | solution.py:37
  2.6 44.2 %collective-permute-start.2 = (bf16[3,96,448]{2,1,0:T(8,128)(2,1)S(1)}, bf16[3,96,448]{2,1,0:T(8,128)(2,1)S(1)}, u32[]{:S(2)}, u32[]{:S(2)}) collective-permute-start(bf16[3,96,448]{2,1,0:T(8,128)(2,1)S(1)} %slice.10), channel_id=1, source_target_pairs={{0,252},{1,253},{2,254},{3,255},{4,0},{252,248},{253,249},{254,250... | collective-permute-start | bytes 774152 | tf_op jit(solution)/shard_map/ppermute | solution.py:37
  46.8 0.1 collective-permute-start.3
  46.9 5.0 %collective-permute-done.3 = s32[1,64,49]{1,0,2:T(1,128)S(1)} collective-permute-done((s32[1,64,49]{1,0,2:T(1,128)S(1)}, s32[1,64,49]{1,0,2:T(1,128)S(1)}, u32[]{:S(2)}, u32[]{:S(2)}) %collective-permute-start.3) | collective-permute-done | bytes 12576 | tf_op jit(solution)/shard_map/ppermute | solution.py:37
  51.9 0.0 collective-permute-done.1.after_main.refs_1_
  52.0 0.0 copy-start.7
  52.0 0.0 copy-start.1
  52.0 0.3 shard_map.82
  52.3 3.6 %collective-permute-start.4 = (bf16[21,8,96]{2,1,0:T(8,128)(2,1)S(1)}, bf16[21,8,96]{2,1,0:T(8,128)(2,1)S(1)}, u32[]{:S(2)}, u32[]{:S(2)}) collective-permute-start(bf16[21,8,96]{2,1,0:T(8,128)(2,1)S(1)} %get-tuple-element.7), channel_id=1, source_target_pairs={{0,1},{1,2},{2,3},{3,0},{4,5},{5,6},{6,7},{7,4},{8,9},{9,10},{10,1... | collective-permute-start | bytes 96776 | tf_op jit(solution)/shard_map/ppermute | solution.py:37
  55.9 0.0 copy-start.2
  55.9 0.0 copy-start.4
  55.9 3.7 %collective-permute-start.5 = (bf16[14,8,96]{2,1,0:T(8,128)(2,1)S(1)}, bf16[14,8,96]{2,1,0:T(8,128)(2,1)S(1)}, u32[]{:S(2)}, u32[]{:S(2)}) collective-permute-start(bf16[14,8,96]{2,1,0:T(8,128)(2,1)S(1)} %get-tuple-element.8), channel_id=1, source_target_pairs={{0,3},{1,0},{2,1},{3,2},{4,7},{5,4},{6,5},{7,6},{8,11},{9,8},{10,9... | collective-permute-start | bytes 64520 | tf_op jit(solution)/shard_map/ppermute | solution.py:37
  59.6 0.0 copy-start.6
  59.6 0.1 copy.9
  59.7 0.5 copy-done.6
  60.3 10.5 %shard_map.83.att_early = f32[4,464,96]{2,1,0:T(8,128)S(1)} custom-call(s32[1]{0:T(128)} %bitcast.late, bf16[7,96,448]{2,1,0:T(8,128)(2,1)S(1)} %bitcast.12, bf16[3,96,448]{2,1,0:T(8,128)(2,1)S(1)} %collective-permute-done.1.after_main.refs_1_, s32[49,1,64]{2,1,0:T(1,128)S(1)} %bitcast.17, bf16[96,288]{1,0:T(8,128)(2,1)S(1)} %copy-done.2, ...), custom_call_target="tpu_custom_call" | custom-call | tf_op jit(solution)/shard_map/pallas_call | solution.py:318
  70.8 0.0 copy-start.5
  70.8 5.8 %shard_map.85.att_b = f32[3,464,96]{2,1,0:T(8,128)S(1)} custom-call(s32[1]{0:T(128)} %bitcast.late, bf16[7,96,448]{2,1,0:T(8,128)(2,1)S(1)} %bitcast.13, bf16[4,96,448]{2,1,0:T(8,128)(2,1)S(1)} %collective-permute-done.before, s32[49,1,64]{2,1,0:T(1,128)S(1)} %bitcast.21, bf16[96,288]{1,0:T(8,128)(2,1)S(1)} %copy-done.2, bf16[96,96]{1,0:T(8,128)(2,1)S(1)} %copy-done.4, ...), custom_call_target="tpu_custom_call" | custom-call | tf_op jit(solution)/shard_map/pallas_call | solution.py:318
  76.6 0.0 collective-permute-done.4.left
  76.6 4.7 %shard_map.86 = bf16[7,96,448]{2,1,0:T(8,128)(2,1)} custom-call(s32[1]{0:T(128)} %bitcast.late, bf16[7,96,448]{2,1,0:T(8,128)(2,1)S(1)} %bitcast.14, bf16[4,96,448]{2,1,0:T(8,128)(2,1)S(1)} %collective-permute-done.before, bf16[3,96,448]{2,1,0:T(8,128)(2,1)S(1)} %collective-permute-done.1.after_main.refs_1_, ...), custom_call_target="tpu_custom_call" | custom-call | tf_op jit(solution)/shard_map/pallas_call | solution.py:318
  (12 shorter events, 0.0 us)
Async XLA Ops:
  0.0 1.2 %copy-start = (bf16[7,448,96]{1,2,0:T(8,128)(2,1)S(1)}, bf16[7,448,96]{1,2,0:T(8,128)(2,1)}, u32[]{:S(2)}) copy-start(bf16[7,448,96]{1,2,0:T(8,128)(2,1)} %param.8) | copy-start | bytes 1806340
  1.1 45.7 %copy-start.3 = (s32[1,64,49]{1,0,2:T(1,128)S(1)}, s32[1,64,49]{1,0,2:T(1,128)}, u32[]{:S(2)}) copy-start(s32[1,64,49]{1,0,2:T(1,128)} %param.9) | copy-start | bytes 37636
  1.1 50.8 %collective-permute-start = (bf16[4,96,448]{2,1,0:T(8,128)(2,1)S(1)}, bf16[4,96,448]{2,1,0:T(8,128)(2,1)S(1)}, u32[]{:S(2)}, u32[]{:S(2)}) collective-permute-start(bf16[4,96,448]{2,1,0:T(8,128)(2,1)S(1)} %slice.9), channel_id=1, source_target_pairs={{0,4},{1,5},{2,6},{3,7},{4,8},{5,9},{6,10},{7,11},{8,12},{9,13},{1... | collective-permute-start | bytes 1032200 | tf_op jit(solution)/shard_map/ppermute | solution.py:37
  1.2 50.7 %collective-permute-start.1 = (bf16[3,96,448]{2,1,0:T(8,128)(2,1)S(1)}, bf16[3,96,448]{2,1,0:T(8,128)(2,1)S(1)}, u32[]{:S(2)}, u32[]{:S(2)}) collective-permute-start(bf16[3,96,448]{2,1,0:T(8,128)(2,1)S(1)} %slice.10), channel_id=1, source_target_pairs={{5,1},{6,2},{7,3},{8,4},{9,5},{10,6},{11,7},{12,8},{13,9},{14,10},... | collective-permute-start | bytes 774152 | tf_op jit(solution)/shard_map/ppermute | solution.py:37
  2.6 49.4 %collective-permute-start.2 = (bf16[3,96,448]{2,1,0:T(8,128)(2,1)S(1)}, bf16[3,96,448]{2,1,0:T(8,128)(2,1)S(1)}, u32[]{:S(2)}, u32[]{:S(2)}) collective-permute-start(bf16[3,96,448]{2,1,0:T(8,128)(2,1)S(1)} %slice.10), channel_id=1, source_target_pairs={{0,252},{1,253},{2,254},{3,255},{4,0},{252,248},{253,249},{254,250... | collective-permute-start | bytes 774152 | tf_op jit(solution)/shard_map/ppermute | solution.py:37
  46.8 5.1 %collective-permute-start.3 = (s32[1,64,49]{1,0,2:T(1,128)S(1)}, s32[1,64,49]{1,0,2:T(1,128)S(1)}, u32[]{:S(2)}, u32[]{:S(2)}) collective-permute-start(s32[1,64,49]{1,0,2:T(1,128)S(1)} %copy-done.3), channel_id=1, source_target_pairs={{0,4},{1,5},{2,6},{3,7},{4,8},{5,9},{6,10},{7,11},{8,12},{9,13},{1... | collective-permute-start | bytes 37640 | tf_op jit(solution)/shard_map/ppermute | solution.py:37
  52.0 7.6 %copy-start.7 = (bf16[96,384]{1,0:T(8,128)(2,1)S(1)}, bf16[96,384]{1,0:T(8,128)(2,1)}, u32[]{:S(2)}) copy-start(bf16[96,384]{1,0:T(8,128)(2,1)} %param.13) | copy-start | bytes 221188
  52.0 7.8 %copy-start.1 = (bf16[169,1024]{1,0:T(8,128)(2,1)S(1)}, bf16[169,1024]{1,0:T(8,128)(2,1)}, u32[]{:S(2)}) copy-start(bf16[169,1024]{1,0:T(8,128)(2,1)} %constant.21.clone.refs_6_.onehot) | copy-start | bytes 1038340
  52.3 24.3 %collective-permute-start.4 = (bf16[21,8,96]{2,1,0:T(8,128)(2,1)S(1)}, bf16[21,8,96]{2,1,0:T(8,128)(2,1)S(1)}, u32[]{:S(2)}, u32[]{:S(2)}) collective-permute-start(bf16[21,8,96]{2,1,0:T(8,128)(2,1)S(1)} %get-tuple-element.7), channel_id=1, source_target_pairs={{0,1},{1,2},{2,3},{3,0},{4,5},{5,6},{6,7},{7,4},{8,9},{9,10},{10,1... | collective-permute-start | bytes 96776 | tf_op jit(solution)/shard_map/ppermute | solution.py:37
  55.9 3.9 %copy-start.2 = (bf16[96,288]{1,0:T(8,128)(2,1)S(1)}, bf16[96,288]{1,0:T(8,128)(2,1)}, u32[]{:S(2)}) copy-start(bf16[96,288]{1,0:T(8,128)(2,1)} %weight.3) | copy-start | bytes 165892
  55.9 3.9 %copy-start.4 = (bf16[96,96]{1,0:T(8,128)(2,1)S(1)}, bf16[96,96]{1,0:T(8,128)(2,1)}, u32[]{:S(2)}) copy-start(bf16[96,96]{1,0:T(8,128)(2,1)} %wproj.3) | copy-start | bytes 55300
  55.9 20.7 %collective-permute-start.5 = (bf16[14,8,96]{2,1,0:T(8,128)(2,1)S(1)}, bf16[14,8,96]{2,1,0:T(8,128)(2,1)S(1)}, u32[]{:S(2)}, u32[]{:S(2)}) collective-permute-start(bf16[14,8,96]{2,1,0:T(8,128)(2,1)S(1)} %get-tuple-element.8), channel_id=1, source_target_pairs={{0,3},{1,0},{2,1},{3,2},{4,7},{5,4},{6,5},{7,6},{8,11},{9,8},{10,9... | collective-permute-start | bytes 64520 | tf_op jit(solution)/shard_map/ppermute | solution.py:37
  59.6 0.7 copy-start.6
  70.8 5.8 %copy-start.5 = (bf16[384,96]{0,1:T(8,128)(2,1)S(1)}, bf16[384,96]{0,1:T(8,128)(2,1)}, u32[]{:S(2)}) copy-start(bf16[384,96]{0,1:T(8,128)(2,1)} %param.14) | copy-start | bytes 221188
